TPU v7x, 32 devices: a whole 2x2x4 slice. The times are simulated.
32 devices in a mesh: parts: 2 (over y), gz: 4 (over z), gy: 2 (over x), lc: 2 (over core).
Axes of the slice: x: 2, y: 2, z: 4, core: 2. Of those that a mesh axis runs over, the one named last changes fastest.
Arguments:
- density: float32 [64, 128, 256], P(('parts', 'gz'), 'gy'), parts along dimension 0, may hold values from 0.05 to 1
- void_mask: int32 [64, 128, 256], P(('parts', 'gz'), 'gy'), parts along dimension 0, may hold values 0 or 1
- fixed_mask: int32 [64, 128, 256], P(('parts', 'gz'), 'gy'), parts along dimension 0, may hold values 0 or 1
- displacement: float32 [2, 3, 64, 128, 256], P('lc', None, ('parts', 'gz'), 'gy'), parts along dimension 2, may hold values from -4 to 4
- load_ratio: int32 [4], P('parts'), parts along dimension 0, may hold values from 1 to 8
Outputs:
- gradient: float32 [64, 128, 256], P(('parts', 'gz'), 'gy'), parts along dimension 0
There are 2 independent parts, one for each index of `parts`. A program takes and returns all parts, laid end to end along the dimension named above; each array names one. Nothing has to cross between parts.
All inputs are finite; a program needn't handle non-finite values. No bound on the sum of `void_mask` or of `fixed_mask` on one device may be relied on, other than what follows from the above.
Results may differ from a plain program's by a relative error of at most 0.0001.
Values sent between devices are 32-bit elements; how exact they have to be, the bound alone decides.
A program may use at most 64 MiB of HBM per device.

v0:
```python
import math

import jax
import jax.numpy as jnp
from jax import lax
from jax.experimental import pallas as pl
from jax.experimental.pallas import tpu as pltpu
from jax.sharding import PartitionSpec as P

MESH = pl.DeviceIdType.MESH
POISSON = 0.3
FACTOR = 1.0 / ((1.0 + POISSON) * (1.0 - 2.0 * POISSON))
LAMBDA = POISSON * FACTOR
SHEAR = (0.5 - POISSON) * FACTOR
W = [2.5 - math.sqrt(d) for d in range(7)]
N_COPIES = 40
CHUNKS = 2
TALL = 32
SHORT = 8


def layer_classes(q0, q1, q2, q4, q5):
    p0 = W[0] * q0 + W[1] * q1 + W[2] * q2 + W[4] * q4 + W[5] * q5
    p1 = W[1] * q0 + W[2] * q1 + W[3] * q2 + W[5] * q4 + W[6] * q5
    p2 = W[4] * q0 + W[5] * q1 + W[6] * q2
    return p0, p1, p2


def lane_index(shape):
    return lax.broadcasted_iota(jnp.int32, shape, len(shape) - 1)


def lane_pair(field, step):
    depth = field.shape[-1]
    lane = lane_index(field.shape)
    after = jnp.where(lane < depth - step, pltpu.roll(field, depth - step, 1), 0.0)
    before = jnp.where(lane >= step, pltpu.roll(field, step, 1), 0.0)
    return after + before


def cone_tiles(ref, layer, row, count):
    window = TALL + 16
    f = [ref[layer + k, pl.ds(row, window), :] for k in range(count + 4)]
    mid = slice(8, 8 + TALL)

    def pair(t, step):
        return (pltpu.roll(t, step, 0) + pltpu.roll(t, window - step, 0))[mid]

    result = []
    for k in range(count):
        x0, x1, x2 = f[k + 2], f[k + 1] + f[k + 3], f[k] + f[k + 4]
        q0 = x0[mid]
        q1 = x1[mid] + pair(x0, 1)
        q2 = pair(x1, 1)
        q4 = x2[mid] + pair(x0, 2)
        q5 = pair(x2, 1) + pair(x1, 2)
        p0, p1, p2 = layer_classes(q0, q1, q2, q4, q5)
        result.append(p0 + lane_pair(p1, 1) + lane_pair(p2, 2))
    return result


def present(position, total, step):
    before = (position >= step).astype(jnp.float32)
    return before + (position + step < total).astype(jnp.float32)


def weight_tile(layer, layers, row, rows, depth):
    shape = (TALL, depth)
    sub = lax.broadcasted_iota(jnp.int32, shape, 0) + row
    spot = jnp.full(shape, layer, jnp.int32)
    nx1, nx2 = present(spot, layers, 1), present(spot, layers, 2)
    ny1, ny2 = present(sub, rows, 1), present(sub, rows, 2)
    one = jnp.ones(shape, jnp.float32)
    p0, p1, p2 = layer_classes(one, nx1 + ny1, nx1 * ny1, nx2 + ny2, nx2 * ny1 + nx1 * ny2)
    lane = lane_index(shape)
    return p0 + present(lane, depth, 1) * p1 + present(lane, depth, 2) * p2


def node_modes(ref, layer, row):
    result = []
    for comp in range(3):
        t = ref[comp, layer, pl.ds(row, SHORT + 8), :]
        depth, window = t.shape[-1], t.shape[0]
        tn = jnp.where(lane_index(t.shape) < depth - 1, pltpu.roll(t, depth - 1, 1), 0.0)
        s, d = t + tn, tn - t
        s0, d0 = s[0:SHORT], d[0:SHORT]
        s1, d1 = pltpu.roll(s, window - 1, 0)[0:SHORT], pltpu.roll(d, window - 1, 0)[0:SHORT]
        result.append((s0 + s1, d0 + d1, s1 - s0, d1 - d0))
    return result


def energy_tile(lower, upper):
    modes = []
    for a, b in zip(lower, upper):
        modes.append(
            {
                "x": b[0] - a[0],
                "z": a[1] + b[1],
                "y": a[2] + b[2],
                "yz": a[3] + b[3],
                "xz": b[1] - a[1],
                "xy": b[2] - a[2],
                "xyz": b[3] - a[3],
            }
        )
    u, v, w = modes
    sq = lambda t: t * t
    trace = sq(u["x"] + v["y"] + w["z"])
    linear = sq(v["xy"] + w["xz"]) + sq(u["xy"] + w["yz"]) + sq(u["xz"] + v["yz"])
    normal = sq(u["x"]) + sq(v["y"]) + sq(w["z"])
    bend = sq(u["xy"]) + sq(u["xz"]) + sq(v["xy"]) + sq(v["yz"]) + sq(w["yz"]) + sq(w["xz"])
    shear = sq(u["y"] + v["x"]) + sq(u["z"] + w["x"]) + sq(v["z"] + w["y"])
    twist = sq(u["yz"] + v["xz"]) + sq(u["yz"] + w["xy"]) + sq(v["xz"] + w["xy"])
    cubic = sq(u["xyz"]) + sq(v["xyz"]) + sq(w["xyz"])
    return (1.0 / 16.0) * (
        LAMBDA * trace
        + (LAMBDA / 3.0) * linear
        + (2.0 * SHEAR) * normal
        + SHEAR * (bend + shear)
        + (SHEAR / 3.0) * twist
        + ((LAMBDA + 4.0 * SHEAR) / 9.0) * cubic
    )


def kernel(
    ratio, density, void, fixed, disp, out,
    moved, extra, fix, col_s, col_r, cor_s, cor_r, cor_x, dens, dead, scale, energy, other, sens,
    local, send, recv,
):
    layers, rows, depth = density.shape
    half = layers // 2
    r, c, h = lax.axis_index("gz"), lax.axis_index("gy"), lax.axis_index("lc")
    nr, nc = lax.axis_size("gz"), lax.axis_size("gy")
    dz = 1 - 2 * h
    mid = pl.ds(8, rows)
    low, high = pl.ds(0, 8), pl.ds(rows + 8, 8)

    def there(step_z, step_y):
        z, y = r + step_z, c + step_y
        return (z >= 0) & (z < nr) & (y >= 0) & (y < nc)

    def remote(index, src, dst, step_z, step_y, core):
        copy = pltpu.make_async_remote_copy(
            src_ref=src, dst_ref=dst, send_sem=send.at[index], recv_sem=recv.at[index],
            device_id={"gz": r + step_z, "gy": c + step_y, "lc": core}, device_id_type=MESH,
        )
        goes, comes = there(step_z, step_y), there(-step_z, -step_y)
        return copy, goes, comes

    def between(index, src, dst, step_z, step_y, giver, taker):
        copy, goes, comes = remote(index, src, dst, step_z, step_y, taker)
        return copy, goes & (h == giver), comes & (h == taker)

    def start(entry):
        copy, goes, _ = entry
        pl.when(goes)(copy.start)

    def arrive(entry):
        copy, _, comes = entry
        pl.when(comes)(copy.wait_recv)

    def left(entry):
        copy, goes, _ = entry
        pl.when(goes)(copy.wait_send)

    l0, b0 = half // 2 * (1 - h), half // 2 * h
    keep = half + 2
    lz, sb = (half + 2) * h, (layers - 2) * (1 - h)
    plane, others = pl.ds(0, rows), pl.ds(1, layers - 1)
    get_disp0 = pltpu.make_async_copy(disp.at[0, :, 0], moved.at[:, 0, plane, :], local.at[0])
    get_fix0 = pltpu.make_async_copy(fixed.at[0], fix.at[0], local.at[1])
    get_disp = pltpu.make_async_copy(
        disp.at[0, :, others], moved.at[:, others, plane, :], local.at[2]
    )
    get_fix = pltpu.make_async_copy(fixed.at[others], fix.at[others], local.at[3])
    get_dens = pltpu.make_async_copy(
        density.at[pl.ds(b0, keep)], dens.at[pl.ds(l0, keep), mid, :], local.at[4]
    )
    get_dead = pltpu.make_async_copy(void.at[pl.ds(half * h, half)], dead, local.at[5])
    for copy in (get_disp0, get_fix0, get_disp, get_fix, get_dens, get_dead):
        copy.start()

    barrier = pltpu.get_barrier_semaphore()
    for step_z in (-1, 0, 1):
        for step_y in (-1, 0, 1):
            for flip in (0, 1):
                if step_z == 0 and step_y == 0 and flip == 0:
                    continue
                core = h if flip == 0 else 1 - h

                @pl.when(there(step_z, step_y))
                def _():
                    pl.semaphore_signal(
                        barrier, inc=1,
                        device_id={"gz": r + step_z, "gy": c + step_y, "lc": core},
                        device_id_type=MESH,
                    )

    span_z = 1 + (r > 0).astype(jnp.int32) + (r < nr - 1).astype(jnp.int32)
    span_y = 1 + (c > 0).astype(jnp.int32) + (c < nc - 1).astype(jnp.int32)

    own, edge = pl.ds(b0, keep), pl.ds(sb, 2)
    top, bottom = pl.ds(rows - 8, 8), pl.ds(0, 8)
    near, far = pl.ds(l0, keep), pl.ds(lz, 2)
    dens_copies = [
        remote(0, density.at[edge], dens.at[far, mid, :], dz, 0, h),
        remote(1, density.at[own, top, :], dens.at[near, low, :], 0, 1, h),
        remote(2, density.at[own, bottom, :], dens.at[near, high, :], 0, -1, h),
        remote(3, density.at[edge, top, :], dens.at[far, low, :], dz, 1, h),
        remote(4, density.at[edge, bottom, :], dens.at[far, high, :], dz, -1, h),
    ]

    def free_layer(i, _):
        free = (1 - fix[i]).astype(jnp.float32)
        for comp in range(3):
            moved[comp, i, plane, :] = moved[comp, i, plane, :] * free
        return 0

    tall = rows // CHUNKS
    chunks = [pl.ds(q * tall, tall) for q in range(CHUNKS)]
    first_layer = [
        [
            between(24 + q, moved.at[:, 0, part, :], extra.at[:, 1, part, :], -1, 0, 0, 1),
            between(28 + q, moved.at[:, 0, part, :], moved.at[:, layers, part, :], -1, 0, 1, 1),
        ]
        for q, part in enumerate(chunks)
    ]
    send_col = remote(6, col_s, col_r, 0, -1, h)
    send_cor = [
        between(7, cor_s, cor_r, -1, -1, 1, 1),
        between(5, cor_s, cor_x, -1, -1, 0, 1),
    ]
    get_disp0.wait()
    get_fix0.wait()
    free_layer(0, 0)
    for comp in range(3):
        cor_s[comp : comp + 1, :] = moved[comp, 0, 0:1, :]
    pl.semaphore_wait(barrier, 2 * span_z * span_y - 1)
    for entry in [*send_cor, *first_layer[-1]]:
        start(entry)
    for pieces in first_layer[-2::-1]:
        for entry in pieces:
            start(entry)
    get_disp.wait()
    get_fix.wait()
    lax.fori_loop(1, layers, free_layer, 0)
    for comp in range(3):
        for i in range(layers):
            col_s[comp, i : i + 1, :] = moved[comp, i, 0:1, :]
    start(send_col)
    for entry in dens_copies:
        start(entry)

    @pl.when(r == nr - 1)
    def _():
        for comp in range(3):
            moved[comp, layers, plane, :] = jnp.zeros((rows, depth), jnp.float32)
            extra[comp, 1, plane, :] = jnp.zeros((rows, depth), jnp.float32)

    @pl.when(c == nc - 1)
    def _():
        col_r[...] = jnp.zeros_like(col_r)

    @pl.when(jnp.logical_not(there(1, 1)))
    def _():
        cor_r[...] = jnp.zeros_like(cor_r)
        cor_x[...] = jnp.zeros_like(cor_x)

    blank = jnp.zeros((8, depth), jnp.float32)
    for ref in (dens, sens):

        @pl.when(c == 0)
        def _():
            for i in range(half + 4):
                ref[i, low, :] = blank

        @pl.when(c == nc - 1)
        def _():
            for i in range(half + 4):
                ref[i, high, :] = blank

        @pl.when(jnp.logical_not(there(-dz, 0)))
        def _():
            for i in range(2):
                ref[lz + i] = jnp.zeros((rows + 16, depth), jnp.float32)

    arrive(send_col)
    for comp in range(3):
        for i in range(layers):
            moved[comp, i, pl.ds(rows, 1), :] = col_r[comp, i : i + 1, :]

    send_own = between(
        23, moved.at[:, layers - 1], extra.at[:, 0], 0, 0, 0, 1
    )
    start(send_own)

    ratio_sum = ratio[0]
    for case in range(1, ratio.shape[0]):
        ratio_sum = ratio_sum + ratio[case]
    total = jnp.full((8, depth), ratio_sum.astype(jnp.float32))
    share = jnp.full((8, depth), ratio[h].astype(jnp.float32)) / total
    share_x = jnp.full((8, depth), ratio[1 - h].astype(jnp.float32)) / total

    def energy_layers(first, count):
        def tile(j, _):
            row = pl.multiple_of(j * SHORT, SHORT)
            lower = node_modes(moved, first, row)
            for k in range(count):
                upper = node_modes(moved, first + k + 1, row)
                energy[first + k, pl.ds(row, SHORT), :] = share * energy_tile(lower, upper)
                lower = upper
            return 0

        lax.fori_loop(0, rows // SHORT, tile, 0)

    give = half * (1 - h)
    swap_a = remote(
        8, energy.at[pl.ds(give, half - 1)], other.at[pl.ds(0, half - 1)], 0, 0, 1 - h
    )
    swap_b = between(
        9, energy.at[pl.ds(half - 1, 1)], other.at[pl.ds(half - 1, 1)], 0, 0, 1, 0
    )
    energy_layers(give, half - 1)
    start(swap_a)
    energy_layers((half - 1) * h, half)
    start(swap_b)

    close, wide = 2 * (1 - h), 2 * h

    def scale_two(j):
        def tile(k, _):
            row = pl.multiple_of(k * TALL, TALL)
            cones = cone_tiles(dens, j, row, 2)
            for n in range(2):
                weights = weight_tile(
                    r * layers + half * h + j + n, nr * layers, c * rows + row, nc * rows, depth
                )
                inverse = 1.0 / weights
                physical = cones[n] * inverse
                alive = (1 - dead[j + n, pl.ds(row, TALL), :]).astype(jnp.float32)
                scale[j + n, pl.ds(row, TALL), :] = (
                    alive * (-3.0 * (1.0 - 0.001)) * physical * physical * inverse
                )
            return 0

        lax.fori_loop(0, rows // TALL, tile, 0)

    def sense(j):
        sens[2 + j, mid, :] = scale[j] * (energy[half * h + j] + other[j])

    get_dens.wait()
    get_dead.wait()
    arrive(dens_copies[1])
    arrive(dens_copies[2])
    scale_two(close)
    arrive(swap_a)
    arrive(swap_b)
    sense(close)
    sense(close + 1)

    ps, pd = pl.ds(half - (half - 2) * h, 2), pl.ds((half + 2) * h, 2)
    zs, zd = pl.ds(2 + (half - 2) * h, 2), pl.ds((half + 2) * (1 - h), 2)
    last, first = pl.ds(rows, 8), pl.ds(8, 8)
    close_copies = [
        remote(10, sens.at[ps, mid, :], sens.at[pd, mid, :], 0, 0, 1 - h),
        remote(12, sens.at[ps, last, :], sens.at[ps, low, :], 0, 1, h),
        remote(13, sens.at[ps, first, :], sens.at[ps, high, :], 0, -1, h),
        remote(14, sens.at[ps, last, :], sens.at[pd, low, :], 0, 1, 1 - h),
        remote(15, sens.at[ps, first, :], sens.at[pd, high, :], 0, -1, 1 - h),
    ]
    for entry in close_copies:
        start(entry)

    for n in (0, 3, 4):
        arrive(dens_copies[n])
    scale_two(wide)
    sense(wide)
    below = between(11, sens.at[pl.ds(2, 2), mid, :], sens.at[pl.ds(half + 2, 2), mid, :], -1, 0, 0, 1)
    above = between(22, sens.at[half, mid, :], sens.at[0, mid, :], 1, 0, 1, 0)
    last_layer = [
        between(
            32 + q,
            sens.at[half + 1, pl.ds(8 + q * tall, tall), :],
            sens.at[1, pl.ds(8 + q * tall, tall), :],
            1, 0, 1, 0,
        )
        for q in range(CHUNKS)
    ]
    start(above)

    @pl.when(h == 0)
    def _():
        sense(1)

    start(below)

    @pl.when(h == 1)
    def _():
        for entry in [*send_cor, send_own]:
            arrive(entry)
        for comp in range(3):
            moved[comp, layers, pl.ds(rows, 1), :] = cor_r[comp : comp + 1, :]
            extra[comp, 1, pl.ds(rows, 1), :] = cor_x[comp : comp + 1, :]
        for q in reversed(range(CHUNKS)):
            for entry in first_layer[q]:
                arrive(entry)

            def tile(k, _):
                row = pl.multiple_of(q * tall + k * SHORT, SHORT)
                here = pl.ds(row, SHORT)
                own = energy_tile(
                    node_modes(moved, layers - 1, row), node_modes(moved, layers, row)
                )
                his = energy_tile(node_modes(extra, 0, row), node_modes(extra, 1, row))
                sens[half + 1, pl.ds(row + 8, SHORT), :] = scale[half - 1, here, :] * (
                    share * own + share_x * his
                )
                return 0

            lax.fori_loop(0, tall // SHORT, tile, 0)
            start(last_layer[q])

    def flipped(index, src, dst, step_y):
        copy, goes, _ = remote(index, src, dst, -dz, step_y, 1 - h)
        return copy, goes, there(-dz, -step_y)

    wide_copies = [
        flipped(16, sens.at[zs, last, :], sens.at[zd, low, :], 1),
        flipped(17, sens.at[zs, first, :], sens.at[zd, high, :], -1),
    ]
    row_copies = [
        remote(18, sens.at[zs, last, :], sens.at[zs, low, :], 0, 1, h),
        remote(19, sens.at[zs, first, :], sens.at[zs, high, :], 0, -1, h),
    ]
    for entry in wide_copies + row_copies:
        start(entry)
    wide_copies = [below, above, *last_layer, *wide_copies]

    def filter_two(j):
        def tile(k, _):
            row = pl.multiple_of(k * TALL, TALL)
            cones = cone_tiles(sens, j, row, 2)
            for n in range(2):
                alive = (1 - dead[j + n, pl.ds(row, TALL), :]).astype(jnp.float32)
                out[half * h + j + n, pl.ds(row, TALL), :] = alive * cones[n]
            return 0

        lax.fori_loop(0, rows // TALL, tile, 0)

    def hand_over(index, j):
        place = pl.ds(half * h + j, 2)
        return remote(index, out.at[place], out.at[place], 0, 0, 1 - h)

    for entry in close_copies + row_copies:
        arrive(entry)
    filter_two(close)
    give_close, give_wide = hand_over(20, close), hand_over(21, wide)
    start(give_close)
    for entry in wide_copies:
        arrive(entry)
    filter_two(wide)
    start(give_wide)
    sent = [*dens_copies, send_col, *send_cor, swap_a, swap_b, send_own]
    for pieces in first_layer:
        sent.extend(pieces)
    for entry in sent + close_copies + wide_copies + row_copies + [give_close, give_wide]:
        left(entry)
    arrive(give_close)
    arrive(give_wide)


def shards(density, void_mask, fixed_mask, displacement, load_ratio):
    layers, rows, depth = density.shape
    half = layers // 2
    f32 = jnp.float32
    hbm = pl.BlockSpec(memory_space=pl.ANY)
    return pl.pallas_call(
        kernel,
        out_shape=pltpu.VMEM(density.shape, f32),
        in_specs=[pl.BlockSpec(memory_space=pltpu.SMEM), hbm, hbm, hbm, hbm],
        out_specs=pl.BlockSpec(memory_space=pltpu.VMEM),
        scratch_shapes=[
            pltpu.VMEM((3, layers + 1, rows + 8, depth), f32),
            pltpu.VMEM((3, 2, rows + 8, depth), f32),
            pltpu.VMEM((layers, rows, depth), jnp.int32),
            pltpu.VMEM((3, layers, depth), f32),
            pltpu.VMEM((3, layers, depth), f32),
            pltpu.VMEM((8, depth), f32),
            pltpu.VMEM((8, depth), f32),
            pltpu.VMEM((8, depth), f32),
            pltpu.VMEM((half + 4, rows + 16, depth), f32),
            pltpu.VMEM((half, rows, depth), jnp.int32),
            pltpu.VMEM((half, rows, depth), f32),
            pltpu.VMEM((layers, rows, depth), f32),
            pltpu.VMEM((half, rows, depth), f32),
            pltpu.VMEM((half + 4, rows + 16, depth), f32),
            pltpu.SemaphoreType.DMA((6,)),
            pltpu.SemaphoreType.DMA((N_COPIES,)),
            pltpu.SemaphoreType.DMA((N_COPIES,)),
        ],
        compiler_params=pltpu.CompilerParams(collective_id=0, has_side_effects=True),
    )(load_ratio, density, void_mask, fixed_mask, displacement)


def solution(mesh):
    placed = (
        P(("parts", "gz"), "gy", None),
        P(("parts", "gz"), "gy", None),
        P(("parts", "gz"), "gy", None),
        P("lc", None, ("parts", "gz"), "gy", None),
        P("parts"),
    )
    return jax.shard_map(
        shards,
        mesh=mesh,
        in_specs=placed,
        out_specs=P(("parts", "gz"), "gy", None),
        check_vma=False,
    )
```

profile of v0, /device:TPU:0, one launch (start us, length us, event | category | flops | bytes accessed | tf_op | source)
XLA Modules:
  0.0 20.4 jit_solution(8001676157976221889)
XLA Ops:
  0.0 19.6 %shard_map.55 = f32[8,64,256]{2,1,0:T(8,128)S(1)} custom-call(s32[2]{0:T(128)} %ratio.1, f32[8,64,256]{2,1,0:T(8,128)} %density.1, s32[8,64,256]{2,1,0:T(8,128)} %void.1, s32[8,64,256]{2,1,0:T(8,128)} %fixed.1, f32[1,3,8,64,256]{4,3,2,1,0:T(8,128)} %disp.1), custom_call_target="tpu_custom_call" | custom-call | tf_op jit(solution)/shard_map/pallas_call | solution.py:477
  19.6 0.8 %copy.7 = f32[8,64,256]{2,1,0:T(8,128)} copy(f32[8,64,256]{2,1,0:T(8,128)S(1)} %shard_map.55) | data formatting | bytes 1048576
where the time goes:
time: 20.5 us; the launch traced here: 20.4 us
  Pallas kernels  19.6 us (96%)
  local copies, waits for them, and re-layouts  0.8 us (4%)
    pallas_call x1, Pallas kernels, shards(): pl.pallas_call(kernel, out_shape=pltpu.VMEM(density.shape, f32), in_specs...  19.6 us
    unnamed x1, local copies, waits for them, and re-layouts  0.8 us

commit v1 on v0

--- a/solution.py
+++ b/solution.py
@@ -13,8 +13,7 @@
 LAMBDA = POISSON * FACTOR
 SHEAR = (0.5 - POISSON) * FACTOR
 W = [2.5 - math.sqrt(d) for d in range(7)]
-N_COPIES = 40
-CHUNKS = 2
+N_COPIES = 32
 TALL = 32
 SHORT = 8
 
@@ -123,8 +122,8 @@
 
 
 def kernel(
-    ratio, density, void, fixed, disp, out,
-    moved, extra, fix, col_s, col_r, cor_s, cor_r, cor_x, dens, dead, scale, energy, other, sens,
+    ratio_in, density, void, fixed, disp, out,
+    moved, fix, col_s, col_r, cor_s, cor_r, dens, dead, scale, energy, other, sens, mine, peer, ratio,
     local, send, recv,
 ):
     layers, rows, depth = density.shape
@@ -139,9 +138,10 @@
         z, y = r + step_z, c + step_y
         return (z >= 0) & (z < nr) & (y >= 0) & (y < nc)
 
-    def remote(index, src, dst, step_z, step_y, core):
+    def remote(index, src, dst, step_z, step_y, core, arrival=None):
         copy = pltpu.make_async_remote_copy(
-            src_ref=src, dst_ref=dst, send_sem=send.at[index], recv_sem=recv.at[index],
+            src_ref=src, dst_ref=dst, send_sem=send.at[index],
+            recv_sem=recv.at[index if arrival is None else arrival],
             device_id={"gz": r + step_z, "gy": c + step_y, "lc": core}, device_id_type=MESH,
         )
         goes, comes = there(step_z, step_y), there(-step_z, -step_y)
@@ -151,6 +151,10 @@
         copy, goes, comes = remote(index, src, dst, step_z, step_y, taker)
         return copy, goes & (h == giver), comes & (h == taker)
 
+    def flipped(index, src, dst, step_y):
+        copy, goes, _ = remote(index, src, dst, -dz, step_y, 1 - h)
+        return copy, goes, there(-dz, -step_y)
+
     def start(entry):
         copy, goes, _ = entry
         pl.when(goes)(copy.start)
@@ -166,18 +170,22 @@
     l0, b0 = half // 2 * (1 - h), half // 2 * h
     keep = half + 2
     lz, sb = (half + 2) * h, (layers - 2) * (1 - h)
-    plane, others = pl.ds(0, rows), pl.ds(1, layers - 1)
-    get_disp0 = pltpu.make_async_copy(disp.at[0, :, 0], moved.at[:, 0, plane, :], local.at[0])
-    get_fix0 = pltpu.make_async_copy(fixed.at[0], fix.at[0], local.at[1])
+    plane = pl.ds(0, rows)
+    given, halo = (layers - 1) * (1 - h), (layers + 1) * h
+    get_disp0 = pltpu.make_async_copy(disp.at[0, :, given], moved.at[:, given + 1, plane, :], local.at[0])
+    get_fix0 = pltpu.make_async_copy(fixed.at[given], fix.at[given], local.at[1])
     get_disp = pltpu.make_async_copy(
-        disp.at[0, :, others], moved.at[:, others, plane, :], local.at[2]
-    )
-    get_fix = pltpu.make_async_copy(fixed.at[others], fix.at[others], local.at[3])
+        disp.at[0, :, pl.ds(h, layers - 1)], moved.at[:, pl.ds(h + 1, layers - 1), plane, :], local.at[2]
+    )
+    get_fix = pltpu.make_async_copy(
+        fixed.at[pl.ds(h, layers - 1)], fix.at[pl.ds(h, layers - 1)], local.at[3]
+    )
     get_dens = pltpu.make_async_copy(
         density.at[pl.ds(b0, keep)], dens.at[pl.ds(l0, keep), mid, :], local.at[4]
     )
     get_dead = pltpu.make_async_copy(void.at[pl.ds(half * h, half)], dead, local.at[5])
-    for copy in (get_disp0, get_fix0, get_disp, get_fix, get_dens, get_dead):
+    get_ratio = pltpu.make_async_copy(ratio_in, ratio, local.at[6])
+    for copy in (get_disp0, get_fix0, get_disp, get_fix, get_ratio, get_dens, get_dead):
         copy.start()
 
     barrier = pltpu.get_barrier_semaphore()
@@ -202,71 +210,72 @@
     own, edge = pl.ds(b0, keep), pl.ds(sb, 2)
     top, bottom = pl.ds(rows - 8, 8), pl.ds(0, 8)
     near, far = pl.ds(l0, keep), pl.ds(lz, 2)
-    dens_copies = [
-        remote(0, density.at[edge], dens.at[far, mid, :], dz, 0, h),
+    dens_rows = [
         remote(1, density.at[own, top, :], dens.at[near, low, :], 0, 1, h),
         remote(2, density.at[own, bottom, :], dens.at[near, high, :], 0, -1, h),
+    ]
+    dens_far = [
+        remote(0, density.at[edge], dens.at[far, mid, :], dz, 0, h),
         remote(3, density.at[edge, top, :], dens.at[far, low, :], dz, 1, h),
         remote(4, density.at[edge, bottom, :], dens.at[far, high, :], dz, -1, h),
     ]
 
-    def free_layer(i, _):
+    def free_layer(i):
         free = (1 - fix[i]).astype(jnp.float32)
         for comp in range(3):
-            moved[comp, i, plane, :] = moved[comp, i, plane, :] * free
-        return 0
-
-    tall = rows // CHUNKS
-    chunks = [pl.ds(q * tall, tall) for q in range(CHUNKS)]
-    first_layer = [
-        [
-            between(24 + q, moved.at[:, 0, part, :], extra.at[:, 1, part, :], -1, 0, 0, 1),
-            between(28 + q, moved.at[:, 0, part, :], moved.at[:, layers, part, :], -1, 0, 1, 1),
-        ]
-        for q, part in enumerate(chunks)
-    ]
+            moved[comp, i + 1, plane, :] = moved[comp, i + 1, plane, :] * free
+
+    send_disp = remote(5, moved.at[:, given + 1, plane, :], moved.at[:, halo, plane, :], dz, 0, h)
     send_col = remote(6, col_s, col_r, 0, -1, h)
-    send_cor = [
-        between(7, cor_s, cor_r, -1, -1, 1, 1),
-        between(5, cor_s, cor_x, -1, -1, 0, 1),
-    ]
+    send_cor = remote(7, cor_s, cor_r, dz, -1, h)
     get_disp0.wait()
     get_fix0.wait()
-    free_layer(0, 0)
+    free_layer(given)
     for comp in range(3):
-        cor_s[comp : comp + 1, :] = moved[comp, 0, 0:1, :]
+        cor_s[comp : comp + 1, :] = moved[comp, given + 1, 0:1, :]
     pl.semaphore_wait(barrier, 2 * span_z * span_y - 1)
-    for entry in [*send_cor, *first_layer[-1]]:
+    start(send_cor)
+    for entry in [send_disp, *dens_rows, *dens_far]:
         start(entry)
-    for pieces in first_layer[-2::-1]:
-        for entry in pieces:
-            start(entry)
     get_disp.wait()
     get_fix.wait()
-    lax.fori_loop(1, layers, free_layer, 0)
+
+    def free_other(i, _):
+        free_layer(i + h)
+        return 0
+
+    lax.fori_loop(0, layers - 1, free_other, 0)
     for comp in range(3):
         for i in range(layers):
-            col_s[comp, i : i + 1, :] = moved[comp, i, 0:1, :]
+            col_s[comp, i : i + 1, :] = moved[comp, i + 1, 0:1, :]
     start(send_col)
-    for entry in dens_copies:
-        start(entry)
+
+    blank = jnp.zeros((8, depth), jnp.float32)
 
     @pl.when(r == nr - 1)
     def _():
         for comp in range(3):
-            moved[comp, layers, plane, :] = jnp.zeros((rows, depth), jnp.float32)
-            extra[comp, 1, plane, :] = jnp.zeros((rows, depth), jnp.float32)
+            moved[comp, layers + 1, plane, :] = jnp.zeros((rows, depth), jnp.float32)
+            moved[comp, layers + 1, pl.ds(rows, 8), :] = blank
 
     @pl.when(c == nc - 1)
     def _():
         col_r[...] = jnp.zeros_like(col_r)
 
-    @pl.when(jnp.logical_not(there(1, 1)))
+    @pl.when(jnp.logical_not(there(-dz, 1)))
     def _():
         cor_r[...] = jnp.zeros_like(cor_r)
-        cor_x[...] = jnp.zeros_like(cor_x)
-
-    blank = jnp.zeros((8, depth), jnp.float32)
+
+    @pl.when(c == 0)
+    def _():
+        mine[low, :] = blank
+        peer[low, :] = blank
+
+    @pl.when(c == nc - 1)
+    def _():
+        mine[high, :] = blank
+        peer[high, :] = blank
+
     for ref in (dens, sens):
 
         @pl.when(c == 0)
@@ -284,34 +293,29 @@
             for i in range(2):
                 ref[lz + i] = jnp.zeros((rows + 16, depth), jnp.float32)
 
-    arrive(send_col)
-    for comp in range(3):
-        for i in range(layers):
-            moved[comp, i, pl.ds(rows, 1), :] = col_r[comp, i : i + 1, :]
-
-    send_own = between(
-        23, moved.at[:, layers - 1], extra.at[:, 0], 0, 0, 0, 1
-    )
-    start(send_own)
-
+    get_ratio.wait()
     ratio_sum = ratio[0]
     for case in range(1, ratio.shape[0]):
         ratio_sum = ratio_sum + ratio[case]
     total = jnp.full((8, depth), ratio_sum.astype(jnp.float32))
     share = jnp.full((8, depth), ratio[h].astype(jnp.float32)) / total
-    share_x = jnp.full((8, depth), ratio[1 - h].astype(jnp.float32)) / total
-
-    def energy_layers(first, count):
+
+    tiles = rows // SHORT
+
+    def energy_rows(first, count, j):
+        row = pl.multiple_of(j * SHORT, SHORT)
+        lower = node_modes(moved, first + 1, row)
+        for k in range(count):
+            upper = node_modes(moved, first + k + 2, row)
+            energy[first + k, pl.ds(row, SHORT), :] = share * energy_tile(lower, upper)
+            lower = upper
+
+    def energy_layers(first, count, end):
         def tile(j, _):
-            row = pl.multiple_of(j * SHORT, SHORT)
-            lower = node_modes(moved, first, row)
-            for k in range(count):
-                upper = node_modes(moved, first + k + 1, row)
-                energy[first + k, pl.ds(row, SHORT), :] = share * energy_tile(lower, upper)
-                lower = upper
+            energy_rows(first, count, j)
             return 0
 
-        lax.fori_loop(0, rows // SHORT, tile, 0)
+        lax.fori_loop(0, end, tile, 0)
 
     give = half * (1 - h)
     swap_a = remote(
@@ -320,9 +324,14 @@
     swap_b = between(
         9, energy.at[pl.ds(half - 1, 1)], other.at[pl.ds(half - 1, 1)], 0, 0, 1, 0
     )
-    energy_layers(give, half - 1)
+    energy_layers(give, half - 1, tiles - 1)
+    arrive(send_col)
+    for comp in range(3):
+        for i in range(layers):
+            moved[comp, i + 1, pl.ds(rows, 1), :] = col_r[comp, i : i + 1, :]
+    energy_rows(give, half - 1, tiles - 1)
     start(swap_a)
-    energy_layers((half - 1) * h, half)
+    energy_layers((half - 1) * h, half, tiles)
     start(swap_b)
 
     close, wide = 2 * (1 - h), 2 * h
@@ -350,8 +359,8 @@
 
     get_dens.wait()
     get_dead.wait()
-    arrive(dens_copies[1])
-    arrive(dens_copies[2])
+    for entry in dens_rows:
+        arrive(entry)
     scale_two(close)
     arrive(swap_a)
     arrive(swap_b)
@@ -371,102 +380,145 @@
     for entry in close_copies:
         start(entry)
 
-    for n in (0, 3, 4):
-        arrive(dens_copies[n])
-    scale_two(wide)
-    sense(wide)
-    below = between(11, sens.at[pl.ds(2, 2), mid, :], sens.at[pl.ds(half + 2, 2), mid, :], -1, 0, 0, 1)
-    above = between(22, sens.at[half, mid, :], sens.at[0, mid, :], 1, 0, 1, 0)
-    last_layer = [
-        between(
-            32 + q,
-            sens.at[half + 1, pl.ds(8 + q * tall, tall), :],
-            sens.at[1, pl.ds(8 + q * tall, tall), :],
-            1, 0, 1, 0,
-        )
-        for q in range(CHUNKS)
-    ]
-    start(above)
-
-    @pl.when(h == 0)
-    def _():
-        sense(1)
-
-    start(below)
-
-    @pl.when(h == 1)
-    def _():
-        for entry in [*send_cor, send_own]:
-            arrive(entry)
-        for comp in range(3):
-            moved[comp, layers, pl.ds(rows, 1), :] = cor_r[comp : comp + 1, :]
-            extra[comp, 1, pl.ds(rows, 1), :] = cor_x[comp : comp + 1, :]
-        for q in reversed(range(CHUNKS)):
-            for entry in first_layer[q]:
-                arrive(entry)
-
-            def tile(k, _):
-                row = pl.multiple_of(q * tall + k * SHORT, SHORT)
-                here = pl.ds(row, SHORT)
-                own = energy_tile(
-                    node_modes(moved, layers - 1, row), node_modes(moved, layers, row)
-                )
-                his = energy_tile(node_modes(extra, 0, row), node_modes(extra, 1, row))
-                sens[half + 1, pl.ds(row + 8, SHORT), :] = scale[half - 1, here, :] * (
-                    share * own + share_x * his
-                )
-                return 0
-
-            lax.fori_loop(0, tall // SHORT, tile, 0)
-            start(last_layer[q])
-
-    def flipped(index, src, dst, step_y):
-        copy, goes, _ = remote(index, src, dst, -dz, step_y, 1 - h)
-        return copy, goes, there(-dz, -step_y)
-
     wide_copies = [
         flipped(16, sens.at[zs, last, :], sens.at[zd, low, :], 1),
         flipped(17, sens.at[zs, first, :], sens.at[zd, high, :], -1),
+        flipped(11, sens.at[zs, mid, :], sens.at[zd, mid, :], 0),
     ]
     row_copies = [
         remote(18, sens.at[zs, last, :], sens.at[zs, low, :], 0, 1, h),
         remote(19, sens.at[zs, first, :], sens.at[zs, high, :], 0, -1, h),
     ]
-    for entry in wide_copies + row_copies:
-        start(entry)
-    wide_copies = [below, above, *last_layer, *wide_copies]
-
-    def filter_two(j):
+    edge_copies = [
+        remote(21, mine.at[last, :], mine.at[low, :], 0, 1, h),
+        remote(22, mine.at[first, :], mine.at[high, :], 0, -1, h),
+        flipped(23, mine.at[last, :], peer.at[low, :], 1),
+        flipped(24, mine.at[first, :], peer.at[high, :], -1),
+        flipped(20, mine.at[mid, :], peer.at[mid, :], 0),
+    ]
+    atop = (r == nr - 1) & (h == 0)
+    whole = energy.at[layers - 1]
+    top_copies = [
+        remote(27, whole.at[plane, :], peer.at[mid, :], 0, 0, 1, 20),
+        remote(25, whole.at[top, :], peer.at[low, :], 0, 1, 1, 23),
+        remote(26, whole.at[bottom, :], peer.at[high, :], 0, -1, 1, 24),
+    ]
+    top_copies = [
+        (copy, goes & atop, comes & (r == nr - 1) & (h == 1)) for copy, goes, comes in top_copies
+    ]
+    joined = (h == 1) | (r > 0)
+    edge_copies[:2] = [(copy, goes & joined, comes & joined) for copy, goes, comes in edge_copies[:2]]
+    arrivals = [top_copies[1], top_copies[2], top_copies[0]]
+    arrivals = [
+        (copy, goes, comes | extra)
+        for (copy, goes, comes), (_, _, extra) in zip(edge_copies[2:], arrivals)
+    ]
+
+    def boundary():
+        @pl.when(atop)
+        def _():
+            energy_layers(layers - 1, 1, tiles)
+
+        for entry in top_copies:
+            start(entry)
+        arrive(send_disp)
+        arrive(send_cor)
+        for comp in range(3):
+            moved[comp, halo, pl.ds(rows, 1), :] = cor_r[comp : comp + 1, :]
+
+        @pl.when(joined)
+        def _():
+            def tile(k, _):
+                row = pl.multiple_of(k * SHORT, SHORT)
+                here = pl.multiple_of(k * SHORT + 8, SHORT)
+                mine[pl.ds(here, SHORT), :] = share * energy_tile(
+                    node_modes(moved, layers * h, row), node_modes(moved, layers * h + 1, row)
+                )
+                return 0
+
+            lax.fori_loop(0, tiles, tile, 0)
+        for entry in edge_copies:
+            start(entry)
+
+    def spread():
+        for entry in dens_far:
+            arrive(entry)
+        scale_two(wide)
+        sense(wide)
+
+        @pl.when(h == 0)
+        def _():
+            sense(1)
+
+        @pl.when(h == 1)
+        def _():
+            sens[half + 1, mid, :] = scale[half - 1]
+
+        for entry in wide_copies + row_copies:
+            start(entry)
+
+    boundary()
+    spread()
+
+    def filter_layers(j, count):
         def tile(k, _):
             row = pl.multiple_of(k * TALL, TALL)
-            cones = cone_tiles(sens, j, row, 2)
-            for n in range(2):
+            cones = cone_tiles(sens, j, row, count)
+            for n in range(count):
                 alive = (1 - dead[j + n, pl.ds(row, TALL), :]).astype(jnp.float32)
                 out[half * h + j + n, pl.ds(row, TALL), :] = alive * cones[n]
             return 0
 
         lax.fori_loop(0, rows // TALL, tile, 0)
 
-    def hand_over(index, j):
-        place = pl.ds(half * h + j, 2)
-        return remote(index, out.at[place], out.at[place], 0, 0, 1 - h)
-
-    for entry in close_copies + row_copies:
+    def hand_over(index, giver, j, count):
+        place = pl.ds(half * giver + j, count)
+        return between(index, out.at[place], out.at[place], 0, 0, giver, 1 - giver)
+
+    early = [hand_over(28, 0, 2, half - 2), hand_over(29, 1, 0, half - 3)]
+    late = [hand_over(30, 0, 0, 2), hand_over(31, 1, half - 3, 3)]
+    for entry in close_copies:
         arrive(entry)
-    filter_two(close)
-    give_close, give_wide = hand_over(20, close), hand_over(21, wide)
-    start(give_close)
+    for entry in row_copies:
+        arrive(entry)
+
+    @pl.when(h == 0)
+    def _():
+        filter_layers(2, half - 2)
+
+    @pl.when(h == 1)
+    def _():
+        filter_layers(0, half - 3)
+
+    for entry in early:
+        start(entry)
     for entry in wide_copies:
         arrive(entry)
-    filter_two(wide)
-    start(give_wide)
-    sent = [*dens_copies, send_col, *send_cor, swap_a, swap_b, send_own]
-    for pieces in first_layer:
-        sent.extend(pieces)
-    for entry in sent + close_copies + wide_copies + row_copies + [give_close, give_wide]:
+    for entry in wide_copies + row_copies:
         left(entry)
-    arrive(give_close)
-    arrive(give_wide)
+    for entry in edge_copies[:2] + arrivals:
+        arrive(entry)
+
+    @pl.when(joined)
+    def _():
+        b = 1 + half * h
+        sens[b] = sens[b] * (mine[...] + peer[...])
+
+    @pl.when(h == 0)
+    def _():
+        filter_layers(0, 2)
+
+    @pl.when(h == 1)
+    def _():
+        filter_layers(half - 3, 3)
+
+    for entry in late:
+        start(entry)
+    sent = [*dens_rows, *dens_far, send_disp, send_col, send_cor, swap_a, swap_b]
+    for entry in sent + close_copies + edge_copies + top_copies + early + late:
+        left(entry)
+    for entry in early + late:
+        arrive(entry)
 
 
 def shards(density, void_mask, fixed_mask, displacement, load_ratio):
@@ -477,15 +529,13 @@
     return pl.pallas_call(
         kernel,
         out_shape=pltpu.VMEM(density.shape, f32),
-        in_specs=[pl.BlockSpec(memory_space=pltpu.SMEM), hbm, hbm, hbm, hbm],
+        in_specs=[hbm] * 5,
         out_specs=pl.BlockSpec(memory_space=pltpu.VMEM),
         scratch_shapes=[
-            pltpu.VMEM((3, layers + 1, rows + 8, depth), f32),
-            pltpu.VMEM((3, 2, rows + 8, depth), f32),
+            pltpu.VMEM((3, layers + 2, rows + 8, depth), f32),
             pltpu.VMEM((layers, rows, depth), jnp.int32),
             pltpu.VMEM((3, layers, depth), f32),
             pltpu.VMEM((3, layers, depth), f32),
-            pltpu.VMEM((8, depth), f32),
             pltpu.VMEM((8, depth), f32),
             pltpu.VMEM((8, depth), f32),
             pltpu.VMEM((half + 4, rows + 16, depth), f32),
@@ -494,7 +544,10 @@
             pltpu.VMEM((layers, rows, depth), f32),
             pltpu.VMEM((half, rows, depth), f32),
             pltpu.VMEM((half + 4, rows + 16, depth), f32),
-            pltpu.SemaphoreType.DMA((6,)),
+            pltpu.VMEM((rows + 16, depth), f32),
+            pltpu.VMEM((rows + 16, depth), f32),
+            pltpu.SMEM(load_ratio.shape, load_ratio.dtype),
+            pltpu.SemaphoreType.DMA((7,)),
             pltpu.SemaphoreType.DMA((N_COPIES,)),
             pltpu.SemaphoreType.DMA((N_COPIES,)),
         ],

time: 20.5 us -> 19.6 us (0.956)
  Pallas kernels: 19.6 us -> 18.7 us
    pallas_call x1, Pallas kernels: 19.6 us -> 18.7 us  [shards(): pl.pallas_call(kernel, out_shape=pltpu.VMEM(density.shape, f32), in_specs...]
where the time goes in v1:
time: 19.6 us; the launch traced here: 19.5 us
  Pallas kernels  18.7 us (95%)
  local copies, waits for them, and re-layouts  0.8 us (4%)
    pallas_call x1, Pallas kernels, shards(): pl.pallas_call(kernel, out_shape=pltpu.VMEM(density.shape, f32), in_specs...  18.7 us
    unnamed x1, local copies, waits for them, and re-layouts  0.8 us

profile of v1, /device:TPU:0, one launch (start us, length us, event | category | flops | bytes accessed | tf_op | source)
XLA Modules:
  0.0 19.5 jit_solution(8375231550785323787)
XLA Ops:
  0.0 18.7 %shard_map.55 = f32[8,64,256]{2,1,0:T(8,128)S(1)} custom-call(s32[2]{0:T(128)} %ratio_in.1, f32[8,64,256]{2,1,0:T(8,128)} %density.1, s32[8,64,256]{2,1,0:T(8,128)} %void.1, s32[8,64,256]{2,1,0:T(8,128)} %fixed.1, f32[1,3,8,64,256]{4,3,2,1,0:T(8,128)} %disp.1), custom_call_target="tpu_custom_call" | custom-call | tf_op jit(solution)/shard_map/pallas_call | solution.py:529
  18.7 0.8 %copy.7 = f32[8,64,256]{2,1,0:T(8,128)} copy(f32[8,64,256]{2,1,0:T(8,128)S(1)} %shard_map.55) | data formatting | bytes 1048576

commit v2 on v1

v2 whole, which is shorter than its diff:
```python
import math

import jax
import jax.numpy as jnp
from jax import lax
from jax.experimental import pallas as pl
from jax.experimental.pallas import tpu as pltpu
from jax.sharding import PartitionSpec as P

MESH = pl.DeviceIdType.MESH
POISSON = 0.3
FACTOR = 1.0 / ((1.0 + POISSON) * (1.0 - 2.0 * POISSON))
LAMBDA = POISSON * FACTOR
SHEAR = (0.5 - POISSON) * FACTOR
RATIO = LAMBDA / SHEAR
W = [2.5 - math.sqrt(d) for d in range(7)]
CHUNKS = 2
N_SEND = 23
N_RECV = 32
TALL = 32
SHORT = 8


def layer_classes(q0, q1, q2, q4, q5):
    p0 = W[0] * q0 + W[1] * q1 + W[2] * q2 + W[4] * q4 + W[5] * q5
    p1 = W[1] * q0 + W[2] * q1 + W[3] * q2 + W[5] * q4 + W[6] * q5
    p2 = W[4] * q0 + W[5] * q1 + W[6] * q2
    return p0, p1, p2


def lane_index(shape):
    return lax.broadcasted_iota(jnp.int32, shape, len(shape) - 1)


def lane_pair(field, step):
    depth = field.shape[-1]
    lane = lane_index(field.shape)
    after = jnp.where(lane < depth - step, pltpu.roll(field, depth - step, 1), 0.0)
    before = jnp.where(lane >= step, pltpu.roll(field, step, 1), 0.0)
    return after + before


def cone_tiles(ref, layer, row, count):
    window = TALL + 16
    f = [ref[layer + k, pl.ds(row, window), :] for k in range(count + 4)]
    mid = slice(8, 8 + TALL)

    def pair(t, step):
        return (pltpu.roll(t, step, 0) + pltpu.roll(t, window - step, 0))[mid]

    result = []
    for k in range(count):
        x0, x1, x2 = f[k + 2], f[k + 1] + f[k + 3], f[k] + f[k + 4]
        q0 = x0[mid]
        q1 = x1[mid] + pair(x0, 1)
        q2 = pair(x1, 1)
        q4 = x2[mid] + pair(x0, 2)
        q5 = pair(x2, 1) + pair(x1, 2)
        p0, p1, p2 = layer_classes(q0, q1, q2, q4, q5)
        result.append(p0 + lane_pair(p1, 1) + lane_pair(p2, 2))
    return result


def present(position, total, step):
    before = (position >= step).astype(jnp.float32)
    return before + (position + step < total).astype(jnp.float32)


def weight_tile(layer, layers, row, rows, depth):
    shape = (TALL, depth)
    sub = lax.broadcasted_iota(jnp.int32, shape, 0) + row
    spot = jnp.full(shape, layer, jnp.int32)
    nx1, nx2 = present(spot, layers, 1), present(spot, layers, 2)
    ny1, ny2 = present(sub, rows, 1), present(sub, rows, 2)
    one = jnp.ones(shape, jnp.float32)
    p0, p1, p2 = layer_classes(one, nx1 + ny1, nx1 * ny1, nx2 + ny2, nx2 * ny1 + nx1 * ny2)
    lane = lane_index(shape)
    return p0 + present(lane, depth, 1) * p1 + present(lane, depth, 2) * p2


def node_modes(ref, layer, row):
    result = []
    for comp in range(3):
        t = ref[comp, layer, pl.ds(row, SHORT + 8), :]
        depth, window = t.shape[-1], t.shape[0]
        here, after = t[0:SHORT], pltpu.roll(t, window - 1, 0)[0:SHORT]
        s, d = here + after, after - here
        inner = lane_index(s.shape) < depth - 1
        sn = jnp.where(inner, pltpu.roll(s, depth - 1, 1), 0.0)
        dn = jnp.where(inner, pltpu.roll(d, depth - 1, 1), 0.0)
        result.append((s + sn, sn - s, d + dn, dn - d))
    return result


def energy_tile(lower, upper):
    modes = []
    for a, b in zip(lower, upper):
        modes.append(
            {
                "x": b[0] - a[0],
                "z": a[1] + b[1],
                "y": a[2] + b[2],
                "yz": a[3] + b[3],
                "xz": b[1] - a[1],
                "xy": b[2] - a[2],
                "xyz": b[3] - a[3],
            }
        )
    u, v, w = modes
    sq = lambda t: t * t
    trace = sq(u["x"] + v["y"] + w["z"])
    normal = sq(u["x"]) + sq(v["y"]) + sq(w["z"])
    bend = sq(u["xy"]) + sq(u["xz"]) + sq(v["xy"]) + sq(v["yz"]) + sq(w["yz"]) + sq(w["xz"])
    cross = v["xy"] * w["xz"] + u["xy"] * w["yz"] + u["xz"] * v["yz"]
    shear = sq(u["y"] + v["x"]) + sq(u["z"] + w["x"]) + sq(v["z"] + w["y"])
    pair = v["xz"] + w["xy"]
    twist = u["yz"] * (u["yz"] + pair) + v["xz"] * pair + sq(w["xy"])
    cubic = sq(u["xyz"]) + sq(v["xyz"]) + sq(w["xyz"])
    return (
        RATIO * trace
        + 2.0 * normal
        + (1.0 + RATIO / 3.0) * bend
        + (2.0 * RATIO / 3.0) * cross
        + shear
        + (2.0 / 3.0) * twist
        + ((RATIO + 4.0) / 9.0) * cubic
    )


def kernel(
    ratio_in, density, void, fixed, disp, out,
    moved, fix, col_s, col_r, cor_s, cor_r, dens, dead, scale, energy, other, sens, mine, peer, ratio,
    local, send, recv, ready,
):
    layers, rows, depth = density.shape
    half = layers // 2
    r, c, h = lax.axis_index("gz"), lax.axis_index("gy"), lax.axis_index("lc")
    nr, nc = lax.axis_size("gz"), lax.axis_size("gy")
    dz = 1 - 2 * h
    mid = pl.ds(8, rows)
    low, high = pl.ds(0, 8), pl.ds(rows + 8, 8)

    def there(step_z, step_y):
        z, y = r + step_z, c + step_y
        return (z >= 0) & (z < nr) & (y >= 0) & (y < nc)

    def remote(index, src, dst, step_z, step_y, core, slot=None):
        copy = pltpu.make_async_remote_copy(
            src_ref=src, dst_ref=dst, send_sem=send.at[index if slot is None else slot],
            recv_sem=recv.at[index],
            device_id={"gz": r + step_z, "gy": c + step_y, "lc": core}, device_id_type=MESH,
        )
        goes, comes = there(step_z, step_y), there(-step_z, -step_y)
        return copy, goes, comes

    def between(index, src, dst, giver, slot=None):
        taker = 1 - giver
        copy, goes, comes = remote(index, src, dst, 0, 0, taker, slot)
        return copy, goes & (h == giver), comes & (h == taker)

    def flipped(index, src, dst, step_y, slot=None):
        copy, goes, _ = remote(index, src, dst, -dz, step_y, 1 - h, slot)
        return copy, goes, there(-dz, -step_y)

    def start(entry, when=True):
        copy, goes, _ = entry
        pl.when(goes & when)(copy.start)

    def arrive(entry):
        copy, _, comes = entry
        pl.when(comes)(copy.wait_recv)

    def left(entry):
        copy, goes, _ = entry
        pl.when(goes)(copy.wait_send)

    l0, b0 = half // 2 * (1 - h), half // 2 * h
    keep = half + 2
    lz, sb = (half + 2) * h, (layers - 2) * (1 - h)
    plane = pl.ds(0, rows)
    given, halo = (layers - 1) * (1 - h), (layers + 1) * h
    get_disp0 = pltpu.make_async_copy(disp.at[0, :, given], moved.at[:, given + 1, plane, :], local.at[0])
    get_fix0 = pltpu.make_async_copy(fixed.at[given], fix.at[given], local.at[1])
    get_disp = pltpu.make_async_copy(
        disp.at[0, :, pl.ds(h, layers - 1)], moved.at[:, pl.ds(h + 1, layers - 1), plane, :], local.at[2]
    )
    get_fix = pltpu.make_async_copy(
        fixed.at[pl.ds(h, layers - 1)], fix.at[pl.ds(h, layers - 1)], local.at[3]
    )
    get_dens = pltpu.make_async_copy(
        density.at[pl.ds(b0, keep)], dens.at[pl.ds(l0, keep), mid, :], local.at[4]
    )
    get_dead = pltpu.make_async_copy(void.at[pl.ds(half * h, half)], dead, local.at[5])
    get_ratio = pltpu.make_async_copy(ratio_in, ratio, local.at[6])
    for copy in (get_disp0, get_fix0, get_disp, get_fix, get_ratio, get_dens, get_dead):
        copy.start()

    barrier = pltpu.get_barrier_semaphore()
    def greet(semaphore, step_z, step_y, core):
        @pl.when(there(step_z, step_y))
        def _():
            pl.semaphore_signal(
                semaphore, inc=1,
                device_id={"gz": r + step_z, "gy": c + step_y, "lc": core},
                device_id_type=MESH,
            )

    flag = lambda held: held.astype(jnp.int32)

    def await_from(semaphore, step_z, step_y, count):
        @pl.when(there(step_z, step_y))
        def _():
            pl.semaphore_wait(semaphore, count)

    for core in (h, 1 - h):
        greet(barrier, 1, 0, core)
        greet(barrier, 0, 1, core)
    greet(barrier, 0, 0, 1 - h)

    own, edge = pl.ds(b0, keep), pl.ds(sb, 2)
    top, bottom = pl.ds(rows - 8, 8), pl.ds(0, 8)
    near, far = pl.ds(l0, keep), pl.ds(lz, 2)
    dens_rows = [
        remote(1, density.at[own, top, :], dens.at[near, low, :], 0, 1, h),
        remote(2, density.at[own, bottom, :], dens.at[near, high, :], 0, -1, h),
    ]
    dens_far = [
        remote(0, density.at[edge], dens.at[far, mid, :], dz, 0, h),
        remote(3, density.at[edge, top, :], dens.at[far, low, :], dz, 1, h),
        remote(4, density.at[edge, bottom, :], dens.at[far, high, :], dz, -1, h),
    ]

    def free_layer(i):
        free = (1 - fix[i]).astype(jnp.float32)
        for comp in range(3):
            moved[comp, i + 1, plane, :] = moved[comp, i + 1, plane, :] * free

    tall = rows // CHUNKS
    parts = [pl.ds(q * tall, tall) for q in range(CHUNKS)]
    send_disp = [
        remote(5 + q, moved.at[:, given + 1, part, :], moved.at[:, halo, part, :], dz, 0, h)
        for q, part in enumerate(parts)
    ]
    send_col = remote(7, col_s, col_r, 0, -1, h)
    send_cor = remote(8, cor_s, cor_r, dz, -1, h)
    pl.semaphore_wait(barrier, 2 * (flag(r > 0) + flag(c > 0)) + 1)
    for core in (h, 1 - h):
        greet(ready.at[0], -1, 0, core)
        greet(ready.at[1], 0, -1, core)
    start(dens_far[0], h == 1)
    start(dens_rows[1])
    get_disp0.wait()
    get_fix0.wait()
    free_layer(given)
    for comp in range(3):
        cor_s[comp : comp + 1, :] = moved[comp, given + 1, 0:1, :]
    get_disp.wait()
    get_fix.wait()

    def free_other(i, _):
        free_layer(i + h)
        return 0

    lax.fori_loop(0, layers - 1, free_other, 0)
    for comp in range(3):
        for i in range(layers):
            col_s[comp, i : i + 1, :] = moved[comp, i + 1, 0:1, :]
    start(send_col)
    await_from(ready.at[0], 1, 0, 2)
    start(dens_far[0], h == 0)
    await_from(ready.at[1], 0, 1, 2)
    start(dens_rows[0])
    for step_y in (-1, 1):
        greet(ready.at[2], 0, step_y, h)

    get_ratio.wait()
    ratio_sum = ratio[0]
    for case in range(1, ratio.shape[0]):
        ratio_sum = ratio_sum + ratio[case]
    total = jnp.full((8, depth), ratio_sum.astype(jnp.float32))
    share = (SHEAR / 16.0) * (jnp.full((8, depth), ratio[h].astype(jnp.float32)) / total)

    tiles = rows // SHORT

    def energy_rows(first, count, j):
        row = pl.multiple_of(j * SHORT, SHORT)
        lower = node_modes(moved, first + 1, row)
        for k in range(count):
            upper = node_modes(moved, first + k + 2, row)
            energy[first + k, pl.ds(row, SHORT), :] = share * energy_tile(lower, upper)
            lower = upper

    def energy_layers(first, count, begin, end):
        def tile(j, _):
            energy_rows(first, count, begin + 2 * j)
            energy_rows(first, count, begin + 2 * j + 1)
            return 0

        lax.fori_loop(0, (end - begin) // 2, tile, 0)

    give = half * (1 - h)
    head = (tiles - 2) * SHORT
    swap_rows = [pl.ds(0, head), pl.ds(head, rows - head)]
    swap_a = [
        remote(
            9 + q, energy.at[pl.ds(give, half - 1), part, :],
            other.at[pl.ds(0, half - 1), part, :], 0, 0, 1 - h,
        )
        for q, part in enumerate(swap_rows)
    ]
    swap_b = [
        between(11 + q, energy.at[half - 1, part, :], other.at[half - 1, part, :], 1)
        for q, part in enumerate(swap_rows)
    ]
    rest = (half - 1) * h
    energy_layers(give, half - 1, 0, tiles - 2)
    start(swap_a[0])
    await_from(ready.at[2], 0, -1, 1)
    await_from(ready.at[2], 0, 1, 1)
    for entry in [*dens_far[1:], send_cor, *send_disp[::-1]]:
        start(entry)
    energy_layers(rest, half, 0, tiles - 2)
    start(swap_b[0])

    blank = jnp.zeros((8, depth), jnp.float32)

    @pl.when(r == nr - 1)
    def _():
        for comp in range(3):
            moved[comp, layers + 1, plane, :] = jnp.zeros((rows, depth), jnp.float32)
            moved[comp, layers + 1, pl.ds(rows, 8), :] = blank

    @pl.when(c == nc - 1)
    def _():
        col_r[...] = jnp.zeros_like(col_r)

    @pl.when(jnp.logical_not(there(-dz, 1)))
    def _():
        cor_r[...] = jnp.zeros_like(cor_r)

    @pl.when(c == 0)
    def _():
        mine[low, :] = blank
        peer[low, :] = blank

    @pl.when(c == nc - 1)
    def _():
        mine[high, :] = blank
        peer[high, :] = blank

    for ref in (dens, sens):

        @pl.when(c == 0)
        def _():
            for i in range(half + 4):
                ref[i, low, :] = blank

        @pl.when(c == nc - 1)
        def _():
            for i in range(half + 4):
                ref[i, high, :] = blank

        @pl.when(jnp.logical_not(there(-dz, 0)))
        def _():
            for i in range(2):
                ref[lz + i] = jnp.zeros((rows + 16, depth), jnp.float32)

    arrive(send_col)
    for comp in range(3):
        for i in range(layers):
            moved[comp, i + 1, pl.ds(rows, 1), :] = col_r[comp, i : i + 1, :]
    energy_layers(give, half - 1, tiles - 2, tiles)
    start(swap_a[1])
    energy_layers(rest, half, tiles - 2, tiles)
    start(swap_b[1])

    close, wide = 2 * (1 - h), 2 * h

    def scale_two(j):
        def tile(k, _):
            row = pl.multiple_of(k * TALL, TALL)
            cones = cone_tiles(dens, j, row, 2)
            for n in range(2):
                weights = weight_tile(
                    r * layers + half * h + j + n, nr * layers, c * rows + row, nc * rows, depth
                )
                inverse = 1.0 / weights
                physical = cones[n] * inverse
                alive = (1 - dead[j + n, pl.ds(row, TALL), :]).astype(jnp.float32)
                scale[j + n, pl.ds(row, TALL), :] = (
                    alive * (-3.0 * (1.0 - 0.001)) * physical * physical * inverse
                )
            return 0

        lax.fori_loop(0, rows // TALL, tile, 0)

    def sense(j):
        sens[2 + j, mid, :] = scale[j] * (energy[half * h + j] + other[j])

    get_dens.wait()
    get_dead.wait()
    for entry in dens_rows:
        arrive(entry)
    scale_two(close)
    for entry in swap_a + swap_b:
        arrive(entry)
    sense(close)
    sense(close + 1)

    ps, pd = pl.ds(half - (half - 2) * h, 2), pl.ds((half + 2) * h, 2)
    zs, zd = pl.ds(2 + (half - 2) * h, 2), pl.ds((half + 2) * (1 - h), 2)
    last, first = pl.ds(rows, 8), pl.ds(8, 8)
    close_copies = [
        remote(13, sens.at[ps, mid, :], sens.at[pd, mid, :], 0, 0, 1 - h),
        remote(14, sens.at[ps, last, :], sens.at[ps, low, :], 0, 1, h),
        remote(15, sens.at[ps, first, :], sens.at[ps, high, :], 0, -1, h),
        remote(16, sens.at[ps, last, :], sens.at[pd, low, :], 0, 1, 1 - h),
        remote(17, sens.at[ps, first, :], sens.at[pd, high, :], 0, -1, 1 - h),
    ]
    for entry in close_copies:
        start(entry)

    wide_copies = [
        flipped(18, sens.at[zs, last, :], sens.at[zd, low, :], 1),
        flipped(19, sens.at[zs, first, :], sens.at[zd, high, :], -1),
        flipped(20, sens.at[zs, mid, :], sens.at[zd, mid, :], 0),
    ]
    row_copies = [
        remote(21, sens.at[zs, last, :], sens.at[zs, low, :], 0, 1, h),
        remote(22, sens.at[zs, first, :], sens.at[zs, high, :], 0, -1, h),
    ]
    edge_copies = [
        remote(23, mine.at[last, :], mine.at[low, :], 0, 1, h, 0),
        remote(24, mine.at[first, :], mine.at[high, :], 0, -1, h, 1),
        flipped(25, mine.at[last, :], peer.at[low, :], 1, 2),
        flipped(26, mine.at[first, :], peer.at[high, :], -1, 3),
    ]
    main_copies = [
        flipped(27 + q, mine.at[pl.ds(8 + q * tall, tall), :], peer.at[pl.ds(8 + q * tall, tall), :], 0, 4 + q)
        for q in range(CHUNKS)
    ]
    atop = (r == nr - 1) & (h == 0)
    whole = energy.at[layers - 1]
    top_copies = [
        remote(25, whole.at[top, :], peer.at[low, :], 0, 1, 1, 6),
        remote(26, whole.at[bottom, :], peer.at[high, :], 0, -1, 1, 7),
        remote(27, whole.at[parts[0], :], peer.at[pl.ds(8, tall), :], 0, 0, 1, 8),
        remote(28, whole.at[parts[1], :], peer.at[pl.ds(8 + tall, tall), :], 0, 0, 1, 9),
    ]
    top_copies = [
        (copy, goes & atop, comes & (r == nr - 1) & (h == 1)) for copy, goes, comes in top_copies
    ]
    joined = (h == 1) | (r > 0)
    edge_copies[:2] = [(copy, goes & joined, comes & joined) for copy, goes, comes in edge_copies[:2]]
    arrivals = [
        (copy, goes, comes | extra)
        for (copy, goes, comes), (_, _, extra) in zip(edge_copies[2:] + main_copies, top_copies)
    ]
    pieces = [
        [edge_copies[1], edge_copies[3], main_copies[0]],
        [edge_copies[0], edge_copies[2], main_copies[1]],
    ]

    def boundary():
        for entry in [*dens_rows, *dens_far, *send_disp, send_col, send_cor, *swap_a, *swap_b]:
            left(entry)

        @pl.when(atop)
        def _():
            energy_layers(layers - 1, 1, 0, tiles)

        for entry in top_copies:
            start(entry)
        arrive(send_cor)
        for comp in range(3):
            moved[comp, halo, pl.ds(rows, 1), :] = cor_r[comp : comp + 1, :]
        for q in reversed(range(CHUNKS)):
            arrive(send_disp[q])

            @pl.when(joined)
            def _():
                for n in range(tall // SHORT):
                    row = q * tall + n * SHORT
                    mine[pl.ds(row + 8, SHORT), :] = share * energy_tile(
                        node_modes(moved, layers * h, row), node_modes(moved, layers * h + 1, row)
                    )

            for entry in pieces[q]:
                start(entry)

    def spread():
        for entry in dens_far:
            arrive(entry)
        scale_two(wide)
        sense(wide)

        @pl.when(h == 0)
        def _():
            sense(1)

        @pl.when(h == 1)
        def _():
            sens[half + 1, mid, :] = scale[half - 1]

        for entry in wide_copies + row_copies:
            start(entry)

    spread()
    boundary()

    def filter_rows(j, count, row):
        cones = cone_tiles(sens, j, row, count)
        for n in range(count):
            alive = (1 - dead[j + n, pl.ds(row, TALL), :]).astype(jnp.float32)
            out[half * h + j + n, pl.ds(row, TALL), :] = alive * cones[n]

    def filter_layers(j, count):
        def tile(k, _):
            filter_rows(j, count, pl.multiple_of(k * TALL, TALL))
            return 0

        lax.fori_loop(0, rows // TALL, tile, 0)

    def hand_over(index, giver, j, count, part):
        place = out.at[pl.ds(half * giver + j, count), part, :]
        return between(index, place, place, giver, index - 19)

    early = [hand_over(29, 0, 2, half - 2, plane), hand_over(29, 1, 0, half - 3, plane)]
    strips = [pl.ds(k * TALL, TALL) for k in range(rows // TALL)]
    late = [
        [hand_over(30 + k, 0, 0, 2, strip), hand_over(30 + k, 1, half - 3, 3, strip)]
        for k, strip in enumerate(strips)
    ]
    for entry in close_copies + row_copies:
        arrive(entry)

    @pl.when(h == 0)
    def _():
        filter_layers(2, half - 2)

    @pl.when(h == 1)
    def _():
        filter_layers(0, half - 3)

    for entry in early:
        start(entry)
    for entry in close_copies + row_copies:
        left(entry)
    for entry in wide_copies:
        arrive(entry)
    for entry in wide_copies:
        left(entry)
    for entry in edge_copies + main_copies + top_copies + early:
        left(entry)
    for entry in edge_copies[:2] + arrivals:
        arrive(entry)

    @pl.when(joined)
    def _():
        b = 1 + half * h
        sens[b] = sens[b] * (mine[...] + peer[...])

    for k in range(rows // TALL):

        @pl.when(h == 0)
        def _():
            filter_rows(0, 2, k * TALL)

        @pl.when(h == 1)
        def _():
            filter_rows(half - 3, 3, k * TALL)

        for entry in late[k]:
            start(entry)
    late = [entry for pair in late for entry in pair]
    for entry in late:
        left(entry)
    for entry in early + late:
        arrive(entry)


def shards(density, void_mask, fixed_mask, displacement, load_ratio):
    layers, rows, depth = density.shape
    half = layers // 2
    f32 = jnp.float32
    hbm = pl.BlockSpec(memory_space=pl.ANY)
    return pl.pallas_call(
        kernel,
        out_shape=pltpu.VMEM(density.shape, f32),
        in_specs=[hbm] * 5,
        out_specs=pl.BlockSpec(memory_space=pltpu.VMEM),
        scratch_shapes=[
            pltpu.VMEM((3, layers + 2, rows + 8, depth), f32),
            pltpu.VMEM((layers, rows, depth), jnp.int32),
            pltpu.VMEM((3, layers, depth), f32),
            pltpu.VMEM((3, layers, depth), f32),
            pltpu.VMEM((8, depth), f32),
            pltpu.VMEM((8, depth), f32),
            pltpu.VMEM((half + 4, rows + 16, depth), f32),
            pltpu.VMEM((half, rows, depth), jnp.int32),
            pltpu.VMEM((half, rows, depth), f32),
            pltpu.VMEM((layers, rows, depth), f32),
            pltpu.VMEM((half, rows, depth), f32),
            pltpu.VMEM((half + 4, rows + 16, depth), f32),
            pltpu.VMEM((rows + 16, depth), f32),
            pltpu.VMEM((rows + 16, depth), f32),
            pltpu.SMEM(load_ratio.shape, load_ratio.dtype),
            pltpu.SemaphoreType.DMA((7,)),
            pltpu.SemaphoreType.DMA((N_SEND,)),
            pltpu.SemaphoreType.DMA((N_RECV,)),
            pltpu.SemaphoreType.REGULAR((3,)),
        ],
        compiler_params=pltpu.CompilerParams(collective_id=0, has_side_effects=True),
    )(load_ratio, density, void_mask, fixed_mask, displacement)


def solution(mesh):
    placed = (
        P(("parts", "gz"), "gy", None),
        P(("parts", "gz"), "gy", None),
        P(("parts", "gz"), "gy", None),
        P("lc", None, ("parts", "gz"), "gy", None),
        P("parts"),
    )
    return jax.shard_map(
        shards,
        mesh=mesh,
        in_specs=placed,
        out_specs=P(("parts", "gz"), "gy", None),
        check_vma=False,
    )
```

time: 19.6 us -> 17.2 us (0.88)
  Pallas kernels: 18.7 us -> 16.2 us
    pallas_call x1, Pallas kernels: 18.7 us -> 16.2 us  [shards(): pl.pallas_call(kernel, out_shape=pltpu.VMEM(density.shape, f32), in_specs...]
where the time goes in v2:
time: 17.2 us; the launch traced here: 17 us
  Pallas kernels  16.2 us (94%)
  local copies, waits for them, and re-layouts  0.8 us (5%)
    pallas_call x1, Pallas kernels, shards(): pl.pallas_call(kernel, out_shape=pltpu.VMEM(density.shape, f32), in_specs...  16.2 us
    unnamed x1, local copies, waits for them, and re-layouts  0.8 us

profile of v2, /device:TPU:0, one launch (start us, length us, event | category | flops | bytes accessed | tf_op | source)
XLA Modules:
  0.0 17.0 jit_solution(3007580604706849404)
XLA Ops:
  0.0 16.2 %shard_map.55 = f32[8,64,256]{2,1,0:T(8,128)S(1)} custom-call(s32[2]{0:T(128)} %ratio_in.1, f32[8,64,256]{2,1,0:T(8,128)} %density.1, s32[8,64,256]{2,1,0:T(8,128)} %void.1, s32[8,64,256]{2,1,0:T(8,128)} %fixed.1, f32[1,3,8,64,256]{4,3,2,1,0:T(8,128)} %disp.1), custom_call_target="tpu_custom_call" | custom-call | tf_op jit(solution)/shard_map/pallas_call | solution.py:587
  16.2 0.8 %copy.7 = f32[8,64,256]{2,1,0:T(8,128)} copy(f32[8,64,256]{2,1,0:T(8,128)S(1)} %shard_map.55) | data formatting | bytes 1048576

commit v3 on v2

--- a/solution.py
+++ b/solution.py
@@ -15,8 +15,9 @@
 RATIO = LAMBDA / SHEAR
 W = [2.5 - math.sqrt(d) for d in range(7)]
 CHUNKS = 2
-N_SEND = 23
-N_RECV = 32
+EDGE = 2
+N_SEND = 22
+N_RECV = 31
 TALL = 32
 SHORT = 8
 
@@ -58,6 +59,31 @@
         q5 = pair(x2, 1) + pair(x1, 2)
         p0, p1, p2 = layer_classes(q0, q1, q2, q4, q5)
         result.append(p0 + lane_pair(p1, 1) + lane_pair(p2, 2))
+    return result
+
+
+def boundary_cones(ref, layer, row, reaches):
+    window = TALL + 16
+    t = ref[layer, pl.ds(row, window), :]
+    mid = slice(8, 8 + TALL)
+    t0 = t[mid]
+    t1, t2 = [
+        (pltpu.roll(t, step, 0) + pltpu.roll(t, window - step, 0))[mid] for step in (1, 2)
+    ]
+    result = []
+    for reach in reaches:
+        if reach == 0:
+            p0 = W[0] * t0 + W[1] * t1 + W[4] * t2
+            p1 = W[1] * t0 + W[2] * t1 + W[5] * t2
+            p2 = W[4] * t0 + W[5] * t1
+        elif reach == 1:
+            p0 = W[1] * t0 + W[2] * t1 + W[5] * t2
+            p1 = W[2] * t0 + W[3] * t1 + W[6] * t2
+            p2 = W[5] * t0 + W[6] * t1
+        else:
+            p0, p1, p2 = W[4] * t0 + W[5] * t1, W[5] * t0 + W[6] * t1, None
+        total = p0 + lane_pair(p1, 1)
+        result.append(total if p2 is None else total + lane_pair(p2, 2))
     return result
 
 
@@ -129,8 +155,8 @@
 
 def kernel(
     ratio_in, density, void, fixed, disp, out,
-    moved, fix, col_s, col_r, cor_s, cor_r, dens, dead, scale, energy, other, sens, mine, peer, ratio,
-    local, send, recv, ready,
+    moved, fix, col_s, col_r, cor_s, cor_r, dens, dead, scale, energy, other, sens, mine, peer, hold, ratio,
+    border, rim, held, local, send, recv, ready,
 ):
     layers, rows, depth = density.shape
     half = layers // 2
@@ -179,20 +205,19 @@
     lz, sb = (half + 2) * h, (layers - 2) * (1 - h)
     plane = pl.ds(0, rows)
     given, halo = (layers - 1) * (1 - h), (layers + 1) * h
-    get_disp0 = pltpu.make_async_copy(disp.at[0, :, given], moved.at[:, given + 1, plane, :], local.at[0])
-    get_fix0 = pltpu.make_async_copy(fixed.at[given], fix.at[given], local.at[1])
     get_disp = pltpu.make_async_copy(
-        disp.at[0, :, pl.ds(h, layers - 1)], moved.at[:, pl.ds(h + 1, layers - 1), plane, :], local.at[2]
+        disp.at[0], moved.at[:, pl.ds(1, layers), plane, :], local.at[0]
     )
-    get_fix = pltpu.make_async_copy(
-        fixed.at[pl.ds(h, layers - 1)], fix.at[pl.ds(h, layers - 1)], local.at[3]
+    get_fix = pltpu.make_async_copy(fixed, fix, local.at[1])
+    get_rim = pltpu.make_async_copy(disp.at[0, :, :, pl.ds(0, 1), :], rim, local.at[6])
+    get_held = pltpu.make_async_copy(fixed.at[:, pl.ds(0, 1), :], held, local.at[7])
+    get_dens = pltpu.make_async_copy(
+        density.at[pl.ds(b0, keep)], dens.at[pl.ds(l0, keep), mid, :], local.at[2]
     )
-    get_dens = pltpu.make_async_copy(
-        density.at[pl.ds(b0, keep)], dens.at[pl.ds(l0, keep), mid, :], local.at[4]
-    )
-    get_dead = pltpu.make_async_copy(void.at[pl.ds(half * h, half)], dead, local.at[5])
-    get_ratio = pltpu.make_async_copy(ratio_in, ratio, local.at[6])
-    for copy in (get_disp0, get_fix0, get_disp, get_fix, get_ratio, get_dens, get_dead):
+    get_dead = pltpu.make_async_copy(void.at[pl.ds(half * h, half)], dead, local.at[3])
+    get_ratio = pltpu.make_async_copy(ratio_in, ratio, local.at[4])
+    get_border = pltpu.make_async_copy(density.at[pl.ds(sb, 2)], border, local.at[5])
+    for copy in (get_rim, get_held, get_border, get_dens, get_disp, get_fix, get_ratio, get_dead):
         copy.start()
 
     barrier = pltpu.get_barrier_semaphore()
@@ -205,7 +230,7 @@
                 device_id_type=MESH,
             )
 
-    flag = lambda held: held.astype(jnp.int32)
+    flag = lambda value: value.astype(jnp.int32)
 
     def await_from(semaphore, step_z, step_y, count):
         @pl.when(there(step_z, step_y))
@@ -217,17 +242,22 @@
         greet(barrier, 0, 1, core)
     greet(barrier, 0, 0, 1 - h)
 
-    own, edge = pl.ds(b0, keep), pl.ds(sb, 2)
-    top, bottom = pl.ds(rows - 8, 8), pl.ds(0, 8)
     near, far = pl.ds(l0, keep), pl.ds(lz, 2)
+    tiles = rows // SHORT
+    head = (tiles - 2) * SHORT
+    swap_rows = [pl.ds(0, head), pl.ds(head, rows - head)]
+    top, bottom = pl.ds(rows - EDGE, EDGE), pl.ds(0, EDGE)
+    above, below = pl.ds(8 - EDGE, EDGE), pl.ds(rows + 8, EDGE)
+    last, first = pl.ds(rows + 8 - EDGE, EDGE), pl.ds(8, EDGE)
     dens_rows = [
-        remote(1, density.at[own, top, :], dens.at[near, low, :], 0, 1, h),
-        remote(2, density.at[own, bottom, :], dens.at[near, high, :], 0, -1, h),
+        remote(1, dens.at[near, last, :], dens.at[near, above, :], 0, 1, h),
+        remote(2, dens.at[near, first, :], dens.at[near, below, :], 0, -1, h),
     ]
     dens_far = [
-        remote(0, density.at[edge], dens.at[far, mid, :], dz, 0, h),
-        remote(3, density.at[edge, top, :], dens.at[far, low, :], dz, 1, h),
-        remote(4, density.at[edge, bottom, :], dens.at[far, high, :], dz, -1, h),
+        remote(0, border.at[:, swap_rows[0], :], dens.at[far, pl.ds(8, head), :], dz, 0, h),
+        remote(3, border.at[:, top, :], dens.at[far, above, :], dz, 1, h),
+        remote(4, border.at[:, bottom, :], dens.at[far, below, :], dz, -1, h),
+        remote(30, border.at[:, swap_rows[1], :], dens.at[far, pl.ds(8 + head, rows - head), :], dz, 0, h, 21),
     ]
 
     def free_layer(i):
@@ -247,31 +277,33 @@
     for core in (h, 1 - h):
         greet(ready.at[0], -1, 0, core)
         greet(ready.at[1], 0, -1, core)
+    get_rim.wait()
+    get_held.wait()
+    for i in range(layers):
+        free = (1 - held[i]).astype(jnp.float32)
+        for comp in range(3):
+            col_s[comp, i : i + 1, :] = rim[comp, i] * free
+    start(send_col)
+    for comp in range(3):
+        cor_s[comp : comp + 1, :] = rim[comp, given] * (1 - held[given]).astype(jnp.float32)
+    get_border.wait()
     start(dens_far[0], h == 1)
+    get_dens.wait()
     start(dens_rows[1])
-    get_disp0.wait()
-    get_fix0.wait()
-    free_layer(given)
-    for comp in range(3):
-        cor_s[comp : comp + 1, :] = moved[comp, given + 1, 0:1, :]
     get_disp.wait()
     get_fix.wait()
 
-    def free_other(i, _):
-        free_layer(i + h)
+    def free_step(i, _):
+        free_layer(i)
         return 0
 
-    lax.fori_loop(0, layers - 1, free_other, 0)
-    for comp in range(3):
-        for i in range(layers):
-            col_s[comp, i : i + 1, :] = moved[comp, i + 1, 0:1, :]
-    start(send_col)
+    lax.fori_loop(0, layers, free_step, 0)
     await_from(ready.at[0], 1, 0, 2)
     start(dens_far[0], h == 0)
     await_from(ready.at[1], 0, 1, 2)
     start(dens_rows[0])
-    for step_y in (-1, 1):
-        greet(ready.at[2], 0, step_y, h)
+    greet(ready.at[3], 0, -1, h)
+    greet(ready.at[2], 0, 1, h)
 
     get_ratio.wait()
     ratio_sum = ratio[0]
@@ -280,7 +312,6 @@
     total = jnp.full((8, depth), ratio_sum.astype(jnp.float32))
     share = (SHEAR / 16.0) * (jnp.full((8, depth), ratio[h].astype(jnp.float32)) / total)
 
-    tiles = rows // SHORT
 
     def energy_rows(first, count, j):
         row = pl.multiple_of(j * SHORT, SHORT)
@@ -298,9 +329,29 @@
 
         lax.fori_loop(0, (end - begin) // 2, tile, 0)
 
+    close, wide = 2 * (1 - h), 2 * h
+
+    def scale_rows(j, row):
+        cones = cone_tiles(dens, j, row, 2)
+        for n in range(2):
+            weights = weight_tile(
+                r * layers + half * h + j + n, nr * layers, c * rows + row, nc * rows, depth
+            )
+            inverse = 1.0 / weights
+            physical = cones[n] * inverse
+            alive = (1 - dead[j + n, pl.ds(row, TALL), :]).astype(jnp.float32)
+            scale[j + n, pl.ds(row, TALL), :] = (
+                alive * (-3.0 * (1.0 - 0.001)) * physical * physical * inverse
+            )
+
+    def scale_two(j):
+        def tile(k, _):
+            scale_rows(j, pl.multiple_of(k * TALL, TALL))
+            return 0
+
+        lax.fori_loop(0, rows // TALL, tile, 0)
+
     give = half * (1 - h)
-    head = (tiles - 2) * SHORT
-    swap_rows = [pl.ds(0, head), pl.ds(head, rows - head)]
     swap_a = [
         remote(
             9 + q, energy.at[pl.ds(give, half - 1), part, :],
@@ -316,11 +367,13 @@
     energy_layers(give, half - 1, 0, tiles - 2)
     start(swap_a[0])
     await_from(ready.at[2], 0, -1, 1)
-    await_from(ready.at[2], 0, 1, 1)
-    for entry in [*dens_far[1:], send_cor, *send_disp[::-1]]:
+    for entry in [dens_far[2], send_cor, dens_far[3], send_disp[1]]:
         start(entry)
     energy_layers(rest, half, 0, tiles - 2)
     start(swap_b[0])
+    await_from(ready.at[3], 0, 1, 1)
+    for entry in [dens_far[1], send_disp[0]]:
+        start(entry)
 
     blank = jnp.zeros((8, depth), jnp.float32)
 
@@ -365,6 +418,10 @@
             for i in range(2):
                 ref[lz + i] = jnp.zeros((rows + 16, depth), jnp.float32)
 
+    get_dead.wait()
+    for entry in dens_rows:
+        arrive(entry)
+    scale_two(close)
     arrive(send_col)
     for comp in range(3):
         for i in range(layers):
@@ -374,78 +431,55 @@
     energy_layers(rest, half, tiles - 2, tiles)
     start(swap_b[1])
 
-    close, wide = 2 * (1 - h), 2 * h
-
-    def scale_two(j):
-        def tile(k, _):
-            row = pl.multiple_of(k * TALL, TALL)
-            cones = cone_tiles(dens, j, row, 2)
-            for n in range(2):
-                weights = weight_tile(
-                    r * layers + half * h + j + n, nr * layers, c * rows + row, nc * rows, depth
-                )
-                inverse = 1.0 / weights
-                physical = cones[n] * inverse
-                alive = (1 - dead[j + n, pl.ds(row, TALL), :]).astype(jnp.float32)
-                scale[j + n, pl.ds(row, TALL), :] = (
-                    alive * (-3.0 * (1.0 - 0.001)) * physical * physical * inverse
-                )
-            return 0
-
-        lax.fori_loop(0, rows // TALL, tile, 0)
-
     def sense(j):
         sens[2 + j, mid, :] = scale[j] * (energy[half * h + j] + other[j])
 
-    get_dens.wait()
-    get_dead.wait()
-    for entry in dens_rows:
-        arrive(entry)
-    scale_two(close)
+    strip_count = rows // TALL
+    arrive(dens_far[0])
+    arrive(dens_far[3])
+    for k in range(strip_count):
+        strip = (k + strip_count - c % strip_count) % strip_count
+        for entry, at in ((dens_far[1], 0), (dens_far[2], strip_count - 1)):
+            copy, goes, comes = entry
+            arrive((copy, goes, comes & (strip == at)))
+        scale_rows(wide, pl.multiple_of(strip * TALL, TALL))
     for entry in swap_a + swap_b:
         arrive(entry)
-    sense(close)
-    sense(close + 1)
 
     ps, pd = pl.ds(half - (half - 2) * h, 2), pl.ds((half + 2) * h, 2)
     zs, zd = pl.ds(2 + (half - 2) * h, 2), pl.ds((half + 2) * (1 - h), 2)
-    last, first = pl.ds(rows, 8), pl.ds(8, 8)
     close_copies = [
         remote(13, sens.at[ps, mid, :], sens.at[pd, mid, :], 0, 0, 1 - h),
-        remote(14, sens.at[ps, last, :], sens.at[ps, low, :], 0, 1, h),
-        remote(15, sens.at[ps, first, :], sens.at[ps, high, :], 0, -1, h),
-        remote(16, sens.at[ps, last, :], sens.at[pd, low, :], 0, 1, 1 - h),
-        remote(17, sens.at[ps, first, :], sens.at[pd, high, :], 0, -1, 1 - h),
-    ]
-    for entry in close_copies:
-        start(entry)
-
+        remote(16, sens.at[ps, last, :], sens.at[pd, above, :], 0, 1, 1 - h),
+        remote(17, sens.at[ps, first, :], sens.at[pd, below, :], 0, -1, 1 - h),
+    ]
     wide_copies = [
-        flipped(18, sens.at[zs, last, :], sens.at[zd, low, :], 1),
-        flipped(19, sens.at[zs, first, :], sens.at[zd, high, :], -1),
+        flipped(18, sens.at[zs, last, :], sens.at[zd, above, :], 1),
+        flipped(19, sens.at[zs, first, :], sens.at[zd, below, :], -1),
         flipped(20, sens.at[zs, mid, :], sens.at[zd, mid, :], 0),
     ]
+    core_rows = pl.ds(2, half)
     row_copies = [
-        remote(21, sens.at[zs, last, :], sens.at[zs, low, :], 0, 1, h),
-        remote(22, sens.at[zs, first, :], sens.at[zs, high, :], 0, -1, h),
+        remote(14, sens.at[core_rows, last, :], sens.at[core_rows, above, :], 0, 1, h),
+        remote(15, sens.at[core_rows, first, :], sens.at[core_rows, below, :], 0, -1, h),
     ]
     edge_copies = [
-        remote(23, mine.at[last, :], mine.at[low, :], 0, 1, h, 0),
-        remote(24, mine.at[first, :], mine.at[high, :], 0, -1, h, 1),
-        flipped(25, mine.at[last, :], peer.at[low, :], 1, 2),
-        flipped(26, mine.at[first, :], peer.at[high, :], -1, 3),
+        remote(21, mine.at[last, :], mine.at[above, :], 0, 1, h, 0),
+        remote(22, mine.at[first, :], mine.at[below, :], 0, -1, h, 1),
+        flipped(23, mine.at[last, :], peer.at[above, :], 1, 2),
+        flipped(24, mine.at[first, :], peer.at[below, :], -1, 3),
     ]
     main_copies = [
-        flipped(27 + q, mine.at[pl.ds(8 + q * tall, tall), :], peer.at[pl.ds(8 + q * tall, tall), :], 0, 4 + q)
+        flipped(25 + q, mine.at[pl.ds(8 + q * tall, tall), :], peer.at[pl.ds(8 + q * tall, tall), :], 0, 4 + q)
         for q in range(CHUNKS)
     ]
     atop = (r == nr - 1) & (h == 0)
     whole = energy.at[layers - 1]
     top_copies = [
-        remote(25, whole.at[top, :], peer.at[low, :], 0, 1, 1, 6),
-        remote(26, whole.at[bottom, :], peer.at[high, :], 0, -1, 1, 7),
-        remote(27, whole.at[parts[0], :], peer.at[pl.ds(8, tall), :], 0, 0, 1, 8),
-        remote(28, whole.at[parts[1], :], peer.at[pl.ds(8 + tall, tall), :], 0, 0, 1, 9),
+        remote(23, whole.at[top, :], peer.at[above, :], 0, 1, 1, 6),
+        remote(24, whole.at[bottom, :], peer.at[below, :], 0, -1, 1, 7),
+        remote(25, whole.at[parts[0], :], peer.at[pl.ds(8, tall), :], 0, 0, 1, 8),
+        remote(26, whole.at[parts[1], :], peer.at[pl.ds(8 + tall, tall), :], 0, 0, 1, 9),
     ]
     top_copies = [
         (copy, goes & atop, comes & (r == nr - 1) & (h == 1)) for copy, goes, comes in top_copies
@@ -489,9 +523,6 @@
                 start(entry)
 
     def spread():
-        for entry in dens_far:
-            arrive(entry)
-        scale_two(wide)
         sense(wide)
 
         @pl.when(h == 0)
@@ -502,7 +533,11 @@
         def _():
             sens[half + 1, mid, :] = scale[half - 1]
 
-        for entry in wide_copies + row_copies:
+        for entry in wide_copies:
+            start(entry)
+        sense(close)
+        sense(close + 1)
+        for entry in close_copies + row_copies:
             start(entry)
 
     spread()
@@ -523,12 +558,12 @@
 
     def hand_over(index, giver, j, count, part):
         place = out.at[pl.ds(half * giver + j, count), part, :]
-        return between(index, place, place, giver, index - 19)
-
-    early = [hand_over(29, 0, 2, half - 2, plane), hand_over(29, 1, 0, half - 3, plane)]
+        return between(index, place, place, giver, index - 17)
+
+    early = [hand_over(27, 0, 2, half - 2, plane), hand_over(27, 1, 0, half - 3, plane)]
     strips = [pl.ds(k * TALL, TALL) for k in range(rows // TALL)]
     late = [
-        [hand_over(30 + k, 0, 0, 2, strip), hand_over(30 + k, 1, half - 3, 3, strip)]
+        [hand_over(28 + k, 0, 0, 2, strip), hand_over(28 + k, 1, half - 3, 3, strip)]
         for k, strip in enumerate(strips)
     ]
     for entry in close_copies + row_copies:
@@ -550,30 +585,59 @@
         arrive(entry)
     for entry in wide_copies:
         left(entry)
-    for entry in edge_copies + main_copies + top_copies + early:
+    for entry in edge_copies + main_copies + top_copies:
         left(entry)
+    b = 1 + half * h
+
+    @pl.when(joined)
+    def _():
+        hold[...] = sens[b]
+        sens[b] = jnp.zeros((rows + 16, depth), jnp.float32)
+
+    def partial_layers(j, count):
+        def tile(k, _):
+            row = pl.multiple_of(k * TALL, TALL)
+            for n, cone in enumerate(cone_tiles(sens, j, row, count)):
+                out[half * h + j + n, pl.ds(row, TALL), :] = cone
+            return 0
+
+        lax.fori_loop(0, rows // TALL, tile, 0)
+
+    @pl.when(h == 0)
+    def _():
+        partial_layers(0, 2)
+
+    @pl.when(h == 1)
+    def _():
+        partial_layers(half - 3, 3)
+
+    def finish_rows(pairs, row):
+        for (j, reach), cone in zip(pairs, boundary_cones(sens, b, row, [p[1] for p in pairs])):
+            alive = (1 - dead[j, pl.ds(row, TALL), :]).astype(jnp.float32)
+            here = pl.ds(row, TALL)
+            out[half * h + j, here, :] = alive * (out[half * h + j, here, :] + cone)
+
     for entry in edge_copies[:2] + arrivals:
         arrive(entry)
 
     @pl.when(joined)
     def _():
-        b = 1 + half * h
-        sens[b] = sens[b] * (mine[...] + peer[...])
+        sens[b] = hold[...] * (mine[...] + peer[...])
 
     for k in range(rows // TALL):
 
         @pl.when(h == 0)
         def _():
-            filter_rows(0, 2, k * TALL)
+            finish_rows([(0, 1), (1, 2)], k * TALL)
 
         @pl.when(h == 1)
         def _():
-            filter_rows(half - 3, 3, k * TALL)
+            finish_rows([(half - 3, 2), (half - 2, 1), (half - 1, 0)], k * TALL)
 
         for entry in late[k]:
             start(entry)
     late = [entry for pair in late for entry in pair]
-    for entry in late:
+    for entry in early + late:
         left(entry)
     for entry in early + late:
         arrive(entry)
@@ -604,11 +668,15 @@
             pltpu.VMEM((half + 4, rows + 16, depth), f32),
             pltpu.VMEM((rows + 16, depth), f32),
             pltpu.VMEM((rows + 16, depth), f32),
+            pltpu.VMEM((rows + 16, depth), f32),
             pltpu.SMEM(load_ratio.shape, load_ratio.dtype),
-            pltpu.SemaphoreType.DMA((7,)),
+            pltpu.VMEM((2, rows, depth), f32),
+            pltpu.VMEM((3, layers, 1, depth), f32),
+            pltpu.VMEM((layers, 1, depth), jnp.int32),
+            pltpu.SemaphoreType.DMA((8,)),
             pltpu.SemaphoreType.DMA((N_SEND,)),
             pltpu.SemaphoreType.DMA((N_RECV,)),
-            pltpu.SemaphoreType.REGULAR((3,)),
+            pltpu.SemaphoreType.REGULAR((4,)),
         ],
         compiler_params=pltpu.CompilerParams(collective_id=0, has_side_effects=True),
     )(load_ratio, density, void_mask, fixed_mask, displacement)

time: 17.2 us -> 16.3 us (0.948)
  Pallas kernels: 16.2 us -> 15.4 us
    pallas_call x1, Pallas kernels: 16.2 us -> 15.4 us  [shards(): pl.pallas_call(kernel, out_shape=pltpu.VMEM(density.shape, f32), in_specs...]
where the time goes in v3:
time: 16.3 us; the launch traced here: 16.2 us
  Pallas kernels  15.4 us (94%)
  local copies, waits for them, and re-layouts  0.8 us (5%)
    pallas_call x1, Pallas kernels, shards(): pl.pallas_call(kernel, out_shape=pltpu.VMEM(density.shape, f32), in_specs...  15.4 us
    unnamed x1, local copies, waits for them, and re-layouts  0.8 us

profile of v3, /device:TPU:0, one launch (start us, length us, event | category | flops | bytes accessed | tf_op | source)
XLA Modules:
  0.0 16.2 jit_solution(13428500343533448016)
XLA Ops:
  0.0 15.4 %shard_map.55 = f32[8,64,256]{2,1,0:T(8,128)S(1)} custom-call(s32[2]{0:T(128)} %ratio_in.1, f32[8,64,256]{2,1,0:T(8,128)} %density.1, s32[8,64,256]{2,1,0:T(8,128)} %void.1, s32[8,64,256]{2,1,0:T(8,128)} %fixed.1, f32[1,3,8,64,256]{4,3,2,1,0:T(8,128)} %disp.1), custom_call_target="tpu_custom_call" | custom-call | tf_op jit(solution)/shard_map/pallas_call | solution.py:651
  15.4 0.8 %copy.7 = f32[8,64,256]{2,1,0:T(8,128)} copy(f32[8,64,256]{2,1,0:T(8,128)S(1)} %shard_map.55) | data formatting | bytes 1048576

commit v4 on v3

--- a/solution.py
+++ b/solution.py
@@ -16,8 +16,8 @@
 W = [2.5 - math.sqrt(d) for d in range(7)]
 CHUNKS = 2
 EDGE = 2
-N_SEND = 22
-N_RECV = 31
+N_SEND = 23
+N_RECV = 32
 TALL = 32
 SHORT = 8
 
@@ -266,7 +266,8 @@
             moved[comp, i + 1, plane, :] = moved[comp, i + 1, plane, :] * free
 
     tall = rows // CHUNKS
-    parts = [pl.ds(q * tall, tall) for q in range(CHUNKS)]
+    parts = [pl.ds(0, tall + SHORT), pl.ds(tall + SHORT, rows - tall - SHORT)]
+    halves = [pl.ds(q * tall, tall) for q in range(CHUNKS)]
     send_disp = [
         remote(5 + q, moved.at[:, given + 1, part, :], moved.at[:, halo, part, :], dz, 0, h)
         for q, part in enumerate(parts)
@@ -291,19 +292,19 @@
     get_dens.wait()
     start(dens_rows[1])
     get_disp.wait()
-    get_fix.wait()
-
-    def free_step(i, _):
-        free_layer(i)
-        return 0
-
-    lax.fori_loop(0, layers, free_step, 0)
     await_from(ready.at[0], 1, 0, 2)
     start(dens_far[0], h == 0)
     await_from(ready.at[1], 0, 1, 2)
     start(dens_rows[0])
     greet(ready.at[3], 0, -1, h)
     greet(ready.at[2], 0, 1, h)
+    get_fix.wait()
+
+    def free_step(i, _):
+        free_layer(i)
+        return 0
+
+    lax.fori_loop(0, layers, free_step, 0)
 
     get_ratio.wait()
     ratio_sum = ratio[0]
@@ -367,12 +368,12 @@
     energy_layers(give, half - 1, 0, tiles - 2)
     start(swap_a[0])
     await_from(ready.at[2], 0, -1, 1)
-    for entry in [dens_far[2], send_cor, dens_far[3], send_disp[1]]:
+    for entry in [dens_far[2], send_cor, dens_far[3], send_disp[0]]:
         start(entry)
     energy_layers(rest, half, 0, tiles - 2)
     start(swap_b[0])
     await_from(ready.at[3], 0, 1, 1)
-    for entry in [dens_far[1], send_disp[0]]:
+    for entry in [dens_far[1], send_disp[1]]:
         start(entry)
 
     blank = jnp.zeros((8, depth), jnp.float32)
@@ -453,10 +454,12 @@
         remote(16, sens.at[ps, last, :], sens.at[pd, above, :], 0, 1, 1 - h),
         remote(17, sens.at[ps, first, :], sens.at[pd, below, :], 0, -1, 1 - h),
     ]
+    low_half, high_half = pl.ds(8, tall), pl.ds(8 + tall, rows - tall)
     wide_copies = [
         flipped(18, sens.at[zs, last, :], sens.at[zd, above, :], 1),
         flipped(19, sens.at[zs, first, :], sens.at[zd, below, :], -1),
-        flipped(20, sens.at[zs, mid, :], sens.at[zd, mid, :], 0),
+        flipped(20, sens.at[zs, low_half, :], sens.at[zd, low_half, :], 0),
+        flipped(31, sens.at[zs, high_half, :], sens.at[zd, high_half, :], 0, 22),
     ]
     core_rows = pl.ds(2, half)
     row_copies = [
@@ -478,8 +481,8 @@
     top_copies = [
         remote(23, whole.at[top, :], peer.at[above, :], 0, 1, 1, 6),
         remote(24, whole.at[bottom, :], peer.at[below, :], 0, -1, 1, 7),
-        remote(25, whole.at[parts[0], :], peer.at[pl.ds(8, tall), :], 0, 0, 1, 8),
-        remote(26, whole.at[parts[1], :], peer.at[pl.ds(8 + tall, tall), :], 0, 0, 1, 9),
+        remote(25, whole.at[halves[0], :], peer.at[pl.ds(8, tall), :], 0, 0, 1, 8),
+        remote(26, whole.at[halves[1], :], peer.at[pl.ds(8 + tall, tall), :], 0, 0, 1, 9),
     ]
     top_copies = [
         (copy, goes & atop, comes & (r == nr - 1) & (h == 1)) for copy, goes, comes in top_copies
@@ -499,16 +502,10 @@
         for entry in [*dens_rows, *dens_far, *send_disp, send_col, send_cor, *swap_a, *swap_b]:
             left(entry)
 
-        @pl.when(atop)
-        def _():
-            energy_layers(layers - 1, 1, 0, tiles)
-
-        for entry in top_copies:
-            start(entry)
         arrive(send_cor)
         for comp in range(3):
             moved[comp, halo, pl.ds(rows, 1), :] = cor_r[comp : comp + 1, :]
-        for q in reversed(range(CHUNKS)):
+        for q in range(CHUNKS):
             arrive(send_disp[q])
 
             @pl.when(joined)
@@ -521,6 +518,15 @@
 
             for entry in pieces[q]:
                 start(entry)
+            if q == 0:
+                start(wide_copies[3], c > 0)
+
+        @pl.when(atop)
+        def _():
+            energy_layers(layers - 1, 1, 0, tiles)
+
+        for entry in top_copies:
+            start(entry)
 
     def spread():
         sense(wide)
@@ -533,8 +539,9 @@
         def _():
             sens[half + 1, mid, :] = scale[half - 1]
 
-        for entry in wide_copies:
+        for entry in wide_copies[:3]:
             start(entry)
+        start(wide_copies[3], c == 0)
         sense(close)
         sense(close + 1)
         for entry in close_copies + row_copies:

time: 16.3 us -> 15.7 us (0.963)
  Pallas kernels: 15.4 us -> 14.8 us
    pallas_call x1, Pallas kernels: 15.4 us -> 14.8 us  [shards(): pl.pallas_call(kernel, out_shape=pltpu.VMEM(density.shape, f32), in_specs...]
where the time goes in v4:
time: 15.7 us; the launch traced here: 15.6 us
  Pallas kernels  14.8 us (94%)
  local copies, waits for them, and re-layouts  0.8 us (5%)
    pallas_call x1, Pallas kernels, shards(): pl.pallas_call(kernel, out_shape=pltpu.VMEM(density.shape, f32), in_specs...  14.8 us
    unnamed x1, local copies, waits for them, and re-layouts  0.8 us

profile of v4, /device:TPU:0, one launch (start us, length us, event | category | flops | bytes accessed | tf_op | source)
XLA Modules:
  0.0 15.6 jit_solution(4194790635221753555)
XLA Ops:
  0.0 14.8 %shard_map.55 = f32[8,64,256]{2,1,0:T(8,128)S(1)} custom-call(s32[2]{0:T(128)} %ratio_in.1, f32[8,64,256]{2,1,0:T(8,128)} %density.1, s32[8,64,256]{2,1,0:T(8,128)} %void.1, s32[8,64,256]{2,1,0:T(8,128)} %fixed.1, f32[1,3,8,64,256]{4,3,2,1,0:T(8,128)} %disp.1), custom_call_target="tpu_custom_call" | custom-call | tf_op jit(solution)/shard_map/pallas_call | solution.py:658
  14.8 0.8 %copy.7 = f32[8,64,256]{2,1,0:T(8,128)} copy(f32[8,64,256]{2,1,0:T(8,128)S(1)} %shard_map.55) | data formatting | bytes 1048576

commit v5 on v4

--- a/solution.py
+++ b/solution.py
@@ -16,8 +16,8 @@
 W = [2.5 - math.sqrt(d) for d in range(7)]
 CHUNKS = 2
 EDGE = 2
-N_SEND = 23
-N_RECV = 32
+N_SEND = 19
+N_RECV = 26
 TALL = 32
 SHORT = 8
 
@@ -243,6 +243,7 @@
     greet(barrier, 0, 0, 1 - h)
 
     near, far = pl.ds(l0, keep), pl.ds(lz, 2)
+    zs, zd = pl.ds(2 + (half - 2) * h, 2), pl.ds((half + 2) * (1 - h), 2)
     tiles = rows // SHORT
     head = (tiles - 2) * SHORT
     swap_rows = [pl.ds(0, head), pl.ds(head, rows - head)]
@@ -254,10 +255,9 @@
         remote(2, dens.at[near, first, :], dens.at[near, below, :], 0, -1, h),
     ]
     dens_far = [
-        remote(0, border.at[:, swap_rows[0], :], dens.at[far, pl.ds(8, head), :], dz, 0, h),
-        remote(3, border.at[:, top, :], dens.at[far, above, :], dz, 1, h),
-        remote(4, border.at[:, bottom, :], dens.at[far, below, :], dz, -1, h),
-        remote(30, border.at[:, swap_rows[1], :], dens.at[far, pl.ds(8 + head, rows - head), :], dz, 0, h, 21),
+        remote(0, border, dens.at[far, mid, :], dz, 0, h),
+        flipped(3, dens.at[zs, last, :], dens.at[zd, above, :], 1),
+        flipped(4, dens.at[zs, first, :], dens.at[zd, below, :], -1),
     ]
 
     def free_layer(i):
@@ -292,12 +292,15 @@
     get_dens.wait()
     start(dens_rows[1])
     get_disp.wait()
+    await_from(ready.at[1], 0, 1, 2)
+    greet(ready.at[2], 0, 1, h)
+    start(dens_rows[0])
+    start(dens_far[1], h == 0)
     await_from(ready.at[0], 1, 0, 2)
+    greet(ready.at[3], 0, -1, h)
+    start(dens_far[2], h == 1)
     start(dens_far[0], h == 0)
-    await_from(ready.at[1], 0, 1, 2)
-    start(dens_rows[0])
-    greet(ready.at[3], 0, -1, h)
-    greet(ready.at[2], 0, 1, h)
+    start(send_cor, h == 0)
     get_fix.wait()
 
     def free_step(i, _):
@@ -305,6 +308,10 @@
         return 0
 
     lax.fori_loop(0, layers, free_step, 0)
+    start(send_disp[0])
+    await_from(ready.at[2], 0, -1, 1)
+    start(dens_far[2], h == 0)
+    start(send_cor, h == 1)
 
     get_ratio.wait()
     ratio_sum = ratio[0]
@@ -355,26 +362,27 @@
     give = half * (1 - h)
     swap_a = [
         remote(
-            9 + q, energy.at[pl.ds(give, half - 1), part, :],
+            9, energy.at[pl.ds(give, half - 1), part, :],
             other.at[pl.ds(0, half - 1), part, :], 0, 0, 1 - h,
         )
         for q, part in enumerate(swap_rows)
     ]
     swap_b = [
-        between(11 + q, energy.at[half - 1, part, :], other.at[half - 1, part, :], 1)
+        between(10, energy.at[half - 1, part, :], other.at[half - 1, part, :], 1)
         for q, part in enumerate(swap_rows)
+    ]
+    swap_whole = [
+        remote(9, energy.at[pl.ds(give, half - 1)], other.at[pl.ds(0, half - 1)], 0, 0, 1 - h),
+        between(10, energy.at[half - 1], other.at[half - 1], 1),
     ]
     rest = (half - 1) * h
     energy_layers(give, half - 1, 0, tiles - 2)
     start(swap_a[0])
-    await_from(ready.at[2], 0, -1, 1)
-    for entry in [dens_far[2], send_cor, dens_far[3], send_disp[0]]:
-        start(entry)
     energy_layers(rest, half, 0, tiles - 2)
     start(swap_b[0])
     await_from(ready.at[3], 0, 1, 1)
-    for entry in [dens_far[1], send_disp[1]]:
-        start(entry)
+    start(dens_far[1], h == 1)
+    start(send_disp[1])
 
     blank = jnp.zeros((8, depth), jnp.float32)
 
@@ -437,61 +445,63 @@
 
     strip_count = rows // TALL
     arrive(dens_far[0])
-    arrive(dens_far[3])
     for k in range(strip_count):
         strip = (k + strip_count - c % strip_count) % strip_count
         for entry, at in ((dens_far[1], 0), (dens_far[2], strip_count - 1)):
             copy, goes, comes = entry
             arrive((copy, goes, comes & (strip == at)))
         scale_rows(wide, pl.multiple_of(strip * TALL, TALL))
-    for entry in swap_a + swap_b:
+    for entry in swap_whole:
         arrive(entry)
 
     ps, pd = pl.ds(half - (half - 2) * h, 2), pl.ds((half + 2) * h, 2)
-    zs, zd = pl.ds(2 + (half - 2) * h, 2), pl.ds((half + 2) * (1 - h), 2)
     close_copies = [
-        remote(13, sens.at[ps, mid, :], sens.at[pd, mid, :], 0, 0, 1 - h),
-        remote(16, sens.at[ps, last, :], sens.at[pd, above, :], 0, 1, 1 - h),
-        remote(17, sens.at[ps, first, :], sens.at[pd, below, :], 0, -1, 1 - h),
+        remote(11, sens.at[ps, mid, :], sens.at[pd, mid, :], 0, 0, 1 - h),
+        remote(14, sens.at[ps, last, :], sens.at[pd, above, :], 0, 1, 1 - h),
+        remote(15, sens.at[ps, first, :], sens.at[pd, below, :], 0, -1, 1 - h),
     ]
     low_half, high_half = pl.ds(8, tall), pl.ds(8 + tall, rows - tall)
     wide_copies = [
-        flipped(18, sens.at[zs, last, :], sens.at[zd, above, :], 1),
-        flipped(19, sens.at[zs, first, :], sens.at[zd, below, :], -1),
-        flipped(20, sens.at[zs, low_half, :], sens.at[zd, low_half, :], 0),
-        flipped(31, sens.at[zs, high_half, :], sens.at[zd, high_half, :], 0, 22),
-    ]
+        flipped(16, sens.at[zs, last, :], sens.at[zd, above, :], 1),
+        flipped(17, sens.at[zs, first, :], sens.at[zd, below, :], -1),
+        flipped(18, sens.at[zs, low_half, :], sens.at[zd, low_half, :], 0),
+        flipped(18, sens.at[zs, high_half, :], sens.at[zd, high_half, :], 0),
+    ]
+    wide_whole = [*wide_copies[:2], flipped(18, sens.at[zs, mid, :], sens.at[zd, mid, :], 0)]
     core_rows = pl.ds(2, half)
     row_copies = [
-        remote(14, sens.at[core_rows, last, :], sens.at[core_rows, above, :], 0, 1, h),
-        remote(15, sens.at[core_rows, first, :], sens.at[core_rows, below, :], 0, -1, h),
+        remote(12, sens.at[core_rows, last, :], sens.at[core_rows, above, :], 0, 1, h),
+        remote(13, sens.at[core_rows, first, :], sens.at[core_rows, below, :], 0, -1, h),
     ]
     edge_copies = [
-        remote(21, mine.at[last, :], mine.at[above, :], 0, 1, h, 0),
-        remote(22, mine.at[first, :], mine.at[below, :], 0, -1, h, 1),
-        flipped(23, mine.at[last, :], peer.at[above, :], 1, 2),
-        flipped(24, mine.at[first, :], peer.at[below, :], -1, 3),
+        remote(19, mine.at[last, :], mine.at[above, :], 0, 1, h, 0),
+        remote(20, mine.at[first, :], mine.at[below, :], 0, -1, h, 1),
+        flipped(21, mine.at[last, :], peer.at[above, :], 1, 2),
+        flipped(22, mine.at[first, :], peer.at[below, :], -1, 3),
     ]
     main_copies = [
-        flipped(25 + q, mine.at[pl.ds(8 + q * tall, tall), :], peer.at[pl.ds(8 + q * tall, tall), :], 0, 4 + q)
+        flipped(23, mine.at[pl.ds(8 + q * tall, tall), :], peer.at[pl.ds(8 + q * tall, tall), :], 0, 4)
         for q in range(CHUNKS)
     ]
+    main_whole = flipped(23, mine.at[mid, :], peer.at[mid, :], 0, 4)
     atop = (r == nr - 1) & (h == 0)
     whole = energy.at[layers - 1]
     top_copies = [
-        remote(23, whole.at[top, :], peer.at[above, :], 0, 1, 1, 6),
-        remote(24, whole.at[bottom, :], peer.at[below, :], 0, -1, 1, 7),
-        remote(25, whole.at[halves[0], :], peer.at[pl.ds(8, tall), :], 0, 0, 1, 8),
-        remote(26, whole.at[halves[1], :], peer.at[pl.ds(8 + tall, tall), :], 0, 0, 1, 9),
+        remote(21, whole.at[top, :], peer.at[above, :], 0, 1, 1, 6),
+        remote(22, whole.at[bottom, :], peer.at[below, :], 0, -1, 1, 7),
+        remote(23, whole.at[halves[0], :], peer.at[pl.ds(8, tall), :], 0, 0, 1, 8),
+        remote(23, whole.at[halves[1], :], peer.at[pl.ds(8 + tall, tall), :], 0, 0, 1, 8),
     ]
     top_copies = [
         (copy, goes & atop, comes & (r == nr - 1) & (h == 1)) for copy, goes, comes in top_copies
     ]
+    top_whole, _, _ = remote(23, whole.at[plane, :], peer.at[mid, :], 0, 0, 1, 8)
+    top_whole = [*top_copies[:2], (top_whole, atop, False)]
     joined = (h == 1) | (r > 0)
     edge_copies[:2] = [(copy, goes & joined, comes & joined) for copy, goes, comes in edge_copies[:2]]
     arrivals = [
         (copy, goes, comes | extra)
-        for (copy, goes, comes), (_, _, extra) in zip(edge_copies[2:] + main_copies, top_copies)
+        for (copy, goes, comes), (_, _, extra) in zip(edge_copies[2:] + [main_whole], top_copies)
     ]
     pieces = [
         [edge_copies[1], edge_copies[3], main_copies[0]],
@@ -499,7 +509,7 @@
     ]
 
     def boundary():
-        for entry in [*dens_rows, *dens_far, *send_disp, send_col, send_cor, *swap_a, *swap_b]:
+        for entry in [*dens_rows, *dens_far, *send_disp, send_col, send_cor, *swap_whole]:
             left(entry)
 
         arrive(send_cor)
@@ -563,44 +573,6 @@
 
         lax.fori_loop(0, rows // TALL, tile, 0)
 
-    def hand_over(index, giver, j, count, part):
-        place = out.at[pl.ds(half * giver + j, count), part, :]
-        return between(index, place, place, giver, index - 17)
-
-    early = [hand_over(27, 0, 2, half - 2, plane), hand_over(27, 1, 0, half - 3, plane)]
-    strips = [pl.ds(k * TALL, TALL) for k in range(rows // TALL)]
-    late = [
-        [hand_over(28 + k, 0, 0, 2, strip), hand_over(28 + k, 1, half - 3, 3, strip)]
-        for k, strip in enumerate(strips)
-    ]
-    for entry in close_copies + row_copies:
-        arrive(entry)
-
-    @pl.when(h == 0)
-    def _():
-        filter_layers(2, half - 2)
-
-    @pl.when(h == 1)
-    def _():
-        filter_layers(0, half - 3)
-
-    for entry in early:
-        start(entry)
-    for entry in close_copies + row_copies:
-        left(entry)
-    for entry in wide_copies:
-        arrive(entry)
-    for entry in wide_copies:
-        left(entry)
-    for entry in edge_copies + main_copies + top_copies:
-        left(entry)
-    b = 1 + half * h
-
-    @pl.when(joined)
-    def _():
-        hold[...] = sens[b]
-        sens[b] = jnp.zeros((rows + 16, depth), jnp.float32)
-
     def partial_layers(j, count):
         def tile(k, _):
             row = pl.multiple_of(k * TALL, TALL)
@@ -610,13 +582,55 @@
 
         lax.fori_loop(0, rows // TALL, tile, 0)
 
+    def hand_over(index, giver, j, count, part):
+        place = out.at[pl.ds(half * giver + j, count), part, :]
+        return between(index, place, place, giver, index - 15)
+
+    early = [hand_over(24, 0, 2, half - 2, plane), hand_over(24, 1, 0, half - 3, plane)]
+    strips = [pl.ds(k * TALL, TALL) for k in range(rows // TALL)]
+    late = [
+        [hand_over(25, 0, 0, 2, strip), hand_over(25, 1, half - 3, 3, strip)]
+        for k, strip in enumerate(strips)
+    ]
+    for entry in close_copies + row_copies:
+        arrive(entry)
+
     @pl.when(h == 0)
     def _():
+        filter_layers(2, half - 2)
+
+    @pl.when(h == 1)
+    def _():
+        filter_layers(0, half - 3)
+
+    for entry in early:
+        start(entry)
+    for entry in close_copies + row_copies + wide_whole:
+        left(entry)
+    b = 1 + half * h
+
+    def set_aside():
+        hold[...] = sens[b]
+        sens[b] = jnp.zeros((rows + 16, depth), jnp.float32)
+
+    @pl.when(h == 1)
+    def _():
+        set_aside()
+        partial_layers(half - 3, 1)
+
+    for entry in wide_whole:
+        arrive(entry)
+    for entry in edge_copies + [main_whole] + top_whole:
+        left(entry)
+    pl.when((h == 0) & joined)(set_aside)
+
+    @pl.when(h == 0)
+    def _():
         partial_layers(0, 2)
 
     @pl.when(h == 1)
     def _():
-        partial_layers(half - 3, 3)
+        partial_layers(half - 2, 2)
 
     def finish_rows(pairs, row):
         for (j, reach), cone in zip(pairs, boundary_cones(sens, b, row, [p[1] for p in pairs])):
@@ -643,7 +657,7 @@
 
         for entry in late[k]:
             start(entry)
-    late = [entry for pair in late for entry in pair]
+    late = [hand_over(25, 0, 0, 2, plane), hand_over(25, 1, half - 3, 3, plane)]
     for entry in early + late:
         left(entry)
     for entry in early + late:

time: 15.7 us -> 15.1 us (0.962)
  Pallas kernels: 14.8 us -> 14.2 us
    pallas_call x1, Pallas kernels: 14.8 us -> 14.2 us  [shards(): pl.pallas_call(kernel, out_shape=pltpu.VMEM(density.shape, f32), in_specs...]
where the time goes in v5:
time: 15.1 us; the launch traced here: 15 us
  Pallas kernels  14.2 us (94%)
  local copies, waits for them, and re-layouts  0.8 us (5%)
    pallas_call x1, Pallas kernels, shards(): pl.pallas_call(kernel, out_shape=pltpu.VMEM(density.shape, f32), in_specs...  14.2 us
    unnamed x1, local copies, waits for them, and re-layouts  0.8 us

profile of v5, /device:TPU:0, one launch (start us, length us, event | category | flops | bytes accessed | tf_op | source)
XLA Modules:
  0.0 15.0 jit_solution(2565226903765881831)
XLA Ops:
  0.0 14.2 %shard_map.55 = f32[8,64,256]{2,1,0:T(8,128)S(1)} custom-call(s32[2]{0:T(128)} %ratio_in.1, f32[8,64,256]{2,1,0:T(8,128)} %density.1, s32[8,64,256]{2,1,0:T(8,128)} %void.1, s32[8,64,256]{2,1,0:T(8,128)} %fixed.1, f32[1,3,8,64,256]{4,3,2,1,0:T(8,128)} %disp.1), custom_call_target="tpu_custom_call" | custom-call | tf_op jit(solution)/shard_map/pallas_call | solution.py:672
  14.2 0.8 %copy.7 = f32[8,64,256]{2,1,0:T(8,128)} copy(f32[8,64,256]{2,1,0:T(8,128)S(1)} %shard_map.55) | data formatting | bytes 1048576

commit v6 on v5

--- a/solution.py
+++ b/solution.py
@@ -160,7 +160,7 @@
 ):
     layers, rows, depth = density.shape
     half = layers // 2
-    r, c, h = lax.axis_index("gz"), lax.axis_index("gy"), lax.axis_index("lc")
+    r, c, h = lax.axis_index("gz"), lax.axis_index("gy"), 1 - lax.axis_index("lc")
     nr, nc = lax.axis_size("gz"), lax.axis_size("gy")
     dz = 1 - 2 * h
     mid = pl.ds(8, rows)
@@ -174,7 +174,7 @@
         copy = pltpu.make_async_remote_copy(
             src_ref=src, dst_ref=dst, send_sem=send.at[index if slot is None else slot],
             recv_sem=recv.at[index],
-            device_id={"gz": r + step_z, "gy": c + step_y, "lc": core}, device_id_type=MESH,
+            device_id={"gz": r + step_z, "gy": c + step_y, "lc": 1 - core}, device_id_type=MESH,
         )
         goes, comes = there(step_z, step_y), there(-step_z, -step_y)
         return copy, goes, comes
@@ -226,7 +226,7 @@
         def _():
             pl.semaphore_signal(
                 semaphore, inc=1,
-                device_id={"gz": r + step_z, "gy": c + step_y, "lc": core},
+                device_id={"gz": r + step_z, "gy": c + step_y, "lc": 1 - core},
                 device_id_type=MESH,
             )
 
@@ -240,7 +240,10 @@
     for core in (h, 1 - h):
         greet(barrier, 1, 0, core)
         greet(barrier, 0, 1, core)
-    greet(barrier, 0, 0, 1 - h)
+
+    @pl.when(h == 1)
+    def _():
+        greet(barrier, 0, 0, 0)
 
     near, far = pl.ds(l0, keep), pl.ds(lz, 2)
     zs, zd = pl.ds(2 + (half - 2) * h, 2), pl.ds((half + 2) * (1 - h), 2)
@@ -274,10 +277,20 @@
     ]
     send_col = remote(7, col_s, col_r, 0, -1, h)
     send_cor = remote(8, cor_s, cor_r, dz, -1, h)
-    pl.semaphore_wait(barrier, 2 * (flag(r > 0) + flag(c > 0)) + 1)
+    awaited = 2 * (flag(r > 0) + flag(c > 0)) + (1 - h)
+
+    @pl.when(awaited > 0)
+    def _():
+        pl.semaphore_wait(barrier, awaited)
+
     for core in (h, 1 - h):
         greet(ready.at[0], -1, 0, core)
         greet(ready.at[1], 0, -1, core)
+
+    @pl.when(h == 0)
+    def _():
+        greet(ready.at[4], 0, 0, 1)
+
     get_rim.wait()
     get_held.wait()
     for i in range(layers):
@@ -318,7 +331,7 @@
     for case in range(1, ratio.shape[0]):
         ratio_sum = ratio_sum + ratio[case]
     total = jnp.full((8, depth), ratio_sum.astype(jnp.float32))
-    share = (SHEAR / 16.0) * (jnp.full((8, depth), ratio[h].astype(jnp.float32)) / total)
+    share = (SHEAR / 16.0) * (jnp.full((8, depth), ratio[1 - h].astype(jnp.float32)) / total)
 
 
     def energy_rows(first, count, j):
@@ -377,6 +390,7 @@
     ]
     rest = (half - 1) * h
     energy_layers(give, half - 1, 0, tiles - 2)
+    pl.when(h == 1)(lambda: pl.semaphore_wait(ready.at[4], 1))
     start(swap_a[0])
     energy_layers(rest, half, 0, tiles - 2)
     start(swap_b[0])
@@ -427,10 +441,6 @@
             for i in range(2):
                 ref[lz + i] = jnp.zeros((rows + 16, depth), jnp.float32)
 
-    get_dead.wait()
-    for entry in dens_rows:
-        arrive(entry)
-    scale_two(close)
     arrive(send_col)
     for comp in range(3):
         for i in range(layers):
@@ -439,6 +449,10 @@
     start(swap_a[1])
     energy_layers(rest, half, tiles - 2, tiles)
     start(swap_b[1])
+    get_dead.wait()
+    for entry in dens_rows:
+        arrive(entry)
+    scale_two(close)
 
     def sense(j):
         sens[2 + j, mid, :] = scale[j] * (energy[half * h + j] + other[j])
@@ -451,8 +465,7 @@
             copy, goes, comes = entry
             arrive((copy, goes, comes & (strip == at)))
         scale_rows(wide, pl.multiple_of(strip * TALL, TALL))
-    for entry in swap_whole:
-        arrive(entry)
+    arrive(swap_whole[0])
 
     ps, pd = pl.ds(half - (half - 2) * h, 2), pl.ds((half + 2) * h, 2)
     close_copies = [
@@ -552,6 +565,7 @@
         for entry in wide_copies[:3]:
             start(entry)
         start(wide_copies[3], c == 0)
+        arrive(swap_whole[1])
         sense(close)
         sense(close + 1)
         for entry in close_copies + row_copies:
@@ -697,7 +711,7 @@
             pltpu.SemaphoreType.DMA((8,)),
             pltpu.SemaphoreType.DMA((N_SEND,)),
             pltpu.SemaphoreType.DMA((N_RECV,)),
-            pltpu.SemaphoreType.REGULAR((4,)),
+            pltpu.SemaphoreType.REGULAR((5,)),
         ],
         compiler_params=pltpu.CompilerParams(collective_id=0, has_side_effects=True),
     )(load_ratio, density, void_mask, fixed_mask, displacement)

time: 15.1 us -> 14.7 us (0.974)
  Pallas kernels: 14.2 us -> 13.8 us
    pallas_call x1, Pallas kernels: 14.2 us -> 13.8 us  [shards(): pl.pallas_call(kernel, out_shape=pltpu.VMEM(density.shape, f32), in_specs...]
where the time goes in v6:
time: 14.7 us; the launch traced here: 14.6 us
  Pallas kernels  13.8 us (94%)
  local copies, waits for them, and re-layouts  0.8 us (5%)
    pallas_call x1, Pallas kernels, shards(): pl.pallas_call(kernel, out_shape=pltpu.VMEM(density.shape, f32), in_specs...  13.8 us
    unnamed x1, local copies, waits for them, and re-layouts  0.8 us

profile of v6, /device:TPU:0, one launch (start us, length us, event | category | flops | bytes accessed | tf_op | source)
XLA Modules:
  0.0 14.6 jit_solution(2094893861949242247)
XLA Ops:
  0.0 13.8 %shard_map.55 = f32[8,64,256]{2,1,0:T(8,128)S(1)} custom-call(s32[2]{0:T(128)} %ratio_in.1, f32[8,64,256]{2,1,0:T(8,128)} %density.1, s32[8,64,256]{2,1,0:T(8,128)} %void.1, s32[8,64,256]{2,1,0:T(8,128)} %fixed.1, f32[1,3,8,64,256]{4,3,2,1,0:T(8,128)} %disp.1), custom_call_target="tpu_custom_call" | custom-call | tf_op jit(solution)/shard_map/pallas_call | solution.py:686
  13.8 0.8 %copy.7 = f32[8,64,256]{2,1,0:T(8,128)} copy(f32[8,64,256]{2,1,0:T(8,128)S(1)} %shard_map.55) | data formatting | bytes 1048576

commit v7 on v6

--- a/solution.py
+++ b/solution.py
@@ -16,6 +16,7 @@
 W = [2.5 - math.sqrt(d) for d in range(7)]
 CHUNKS = 2
 EDGE = 2
+UNROLL = 6
 N_SEND = 19
 N_RECV = 26
 TALL = 32
@@ -269,8 +270,9 @@
             moved[comp, i + 1, plane, :] = moved[comp, i + 1, plane, :] * free
 
     tall = rows // CHUNKS
-    parts = [pl.ds(0, tall + SHORT), pl.ds(tall + SHORT, rows - tall - SHORT)]
-    halves = [pl.ds(q * tall, tall) for q in range(CHUNKS)]
+    split = tall - SHORT
+    spans = [(0, split), (split, rows - split)]
+    parts = [pl.ds(0, split + SHORT), pl.ds(split + SHORT, rows - split - SHORT)]
     send_disp = [
         remote(5 + q, moved.at[:, given + 1, part, :], moved.at[:, halo, part, :], dz, 0, h)
         for q, part in enumerate(parts)
@@ -343,12 +345,14 @@
             lower = upper
 
     def energy_layers(first, count, begin, end):
+        step = math.gcd(end - begin, UNROLL)
+
         def tile(j, _):
-            energy_rows(first, count, begin + 2 * j)
-            energy_rows(first, count, begin + 2 * j + 1)
+            for n in range(step):
+                energy_rows(first, count, begin + step * j + n)
             return 0
 
-        lax.fori_loop(0, (end - begin) // 2, tile, 0)
+        lax.fori_loop(0, (end - begin) // step, tile, 0)
 
     close, wide = 2 * (1 - h), 2 * h
 
@@ -493,8 +497,8 @@
         flipped(22, mine.at[first, :], peer.at[below, :], -1, 3),
     ]
     main_copies = [
-        flipped(23, mine.at[pl.ds(8 + q * tall, tall), :], peer.at[pl.ds(8 + q * tall, tall), :], 0, 4)
-        for q in range(CHUNKS)
+        flipped(23, mine.at[pl.ds(8 + begin, size), :], peer.at[pl.ds(8 + begin, size), :], 0, 4)
+        for begin, size in spans
     ]
     main_whole = flipped(23, mine.at[mid, :], peer.at[mid, :], 0, 4)
     atop = (r == nr - 1) & (h == 0)
@@ -502,8 +506,8 @@
     top_copies = [
         remote(21, whole.at[top, :], peer.at[above, :], 0, 1, 1, 6),
         remote(22, whole.at[bottom, :], peer.at[below, :], 0, -1, 1, 7),
-        remote(23, whole.at[halves[0], :], peer.at[pl.ds(8, tall), :], 0, 0, 1, 8),
-        remote(23, whole.at[halves[1], :], peer.at[pl.ds(8 + tall, tall), :], 0, 0, 1, 8),
+        remote(23, whole.at[pl.ds(0, split), :], peer.at[pl.ds(8, split), :], 0, 0, 1, 8),
+        remote(23, whole.at[pl.ds(split, rows - split), :], peer.at[pl.ds(8 + split, rows - split), :], 0, 0, 1, 8),
     ]
     top_copies = [
         (copy, goes & atop, comes & (r == nr - 1) & (h == 1)) for copy, goes, comes in top_copies
@@ -533,8 +537,8 @@
 
             @pl.when(joined)
             def _():
-                for n in range(tall // SHORT):
-                    row = q * tall + n * SHORT
+                begin, size = spans[q]
+                for row in range(begin, begin + size, SHORT):
                     mine[pl.ds(row + 8, SHORT), :] = share * energy_tile(
                         node_modes(moved, layers * h, row), node_modes(moved, layers * h + 1, row)
                     )
@@ -587,11 +591,13 @@
 
         lax.fori_loop(0, rows // TALL, tile, 0)
 
+    def partial_rows(j, count, row):
+        for n, cone in enumerate(cone_tiles(sens, j, row, count)):
+            out[half * h + j + n, pl.ds(row, TALL), :] = cone
+
     def partial_layers(j, count):
         def tile(k, _):
-            row = pl.multiple_of(k * TALL, TALL)
-            for n, cone in enumerate(cone_tiles(sens, j, row, count)):
-                out[half * h + j + n, pl.ds(row, TALL), :] = cone
+            partial_rows(j, count, pl.multiple_of(k * TALL, TALL))
             return 0
 
         lax.fori_loop(0, rows // TALL, tile, 0)
@@ -606,37 +612,45 @@
         [hand_over(25, 0, 0, 2, strip), hand_over(25, 1, half - 3, 3, strip)]
         for k, strip in enumerate(strips)
     ]
-    for entry in close_copies + row_copies:
+    for entry in [*close_copies[:2], row_copies[0]]:
         arrive(entry)
-
-    @pl.when(h == 0)
-    def _():
-        filter_layers(2, half - 2)
-
-    @pl.when(h == 1)
-    def _():
-        filter_layers(0, half - 3)
-
-    for entry in early:
-        start(entry)
     for entry in close_copies + row_copies + wide_whole:
         left(entry)
     b = 1 + half * h
 
-    def set_aside():
-        hold[...] = sens[b]
-        sens[b] = jnp.zeros((rows + 16, depth), jnp.float32)
-
-    @pl.when(h == 1)
-    def _():
-        set_aside()
-        partial_layers(half - 3, 1)
-
+    def set_aside(part):
+        hold[part, :] = sens[b, part, :]
+        sens[b, part, :] = jnp.zeros((part.size, depth), jnp.float32)
+
+    upper, rim_rows = pl.ds(0, rows + 8), pl.ds(rows + 8, 8)
+    pl.when(h == 1)(lambda: set_aside(upper))
+
+    def early_rows(row):
+        @pl.when(h == 0)
+        def _():
+            filter_rows(2, half - 2, row)
+
+        @pl.when(h == 1)
+        def _():
+            filter_rows(0, half - 3, row)
+            partial_rows(half - 3, 1, row)
+
+    for k in range(rows // TALL - 1):
+        early_rows(k * TALL)
+    for entry in [close_copies[2], row_copies[1]]:
+        arrive(entry)
+    pl.when(h == 1)(lambda: set_aside(rim_rows))
+    early_rows(rows - TALL)
+    for entry in early:
+        start(entry)
     for entry in wide_whole:
         arrive(entry)
     for entry in edge_copies + [main_whole] + top_whole:
         left(entry)
-    pl.when((h == 0) & joined)(set_aside)
+    @pl.when((h == 0) & joined)
+    def _():
+        set_aside(upper)
+        set_aside(rim_rows)
 
     @pl.when(h == 0)
     def _():

time: 14.7 us -> 14.6 us (level)
  no operation moved by 1% of the time
where the time goes in v7:
time: 14.6 us; the launch traced here: 14.5 us
  Pallas kernels  13.7 us (94%)
  local copies, waits for them, and re-layouts  0.8 us (5%)
    pallas_call x1, Pallas kernels, shards(): pl.pallas_call(kernel, out_shape=pltpu.VMEM(density.shape, f32), in_specs...  13.7 us
    unnamed x1, local copies, waits for them, and re-layouts  0.8 us

profile of v7, /device:TPU:0, one launch (start us, length us, event | category | flops | bytes accessed | tf_op | source)
XLA Modules:
  0.0 14.5 jit_solution(1543617306861144652)
XLA Ops:
  0.0 13.7 %shard_map.55 = f32[8,64,256]{2,1,0:T(8,128)S(1)} custom-call(s32[2]{0:T(128)} %ratio_in.1, f32[8,64,256]{2,1,0:T(8,128)} %density.1, s32[8,64,256]{2,1,0:T(8,128)} %void.1, s32[8,64,256]{2,1,0:T(8,128)} %fixed.1, f32[1,3,8,64,256]{4,3,2,1,0:T(8,128)} %disp.1), custom_call_target="tpu_custom_call" | custom-call | tf_op jit(solution)/shard_map/pallas_call | solution.py:700
  13.7 0.8 %copy.7 = f32[8,64,256]{2,1,0:T(8,128)} copy(f32[8,64,256]{2,1,0:T(8,128)S(1)} %shard_map.55) | data formatting | bytes 1048576
